TPU v7x, 32 devices: a 4x4x1 block of a 4x4x8 slice. The times are simulated.
32 devices in a mesh: part: 1 (over z), data: 4 (over y), seq: 8 (over x, core).
Axes of the slice: x: 4, y: 4, z: 1, core: 2. Of those that a mesh axis runs over, the one named last changes fastest.
The devices are a block of a 4x4x8 slice.
Arguments:
- enc_out: bfloat16 [128, 64, 512], P(('part', 'data'), 'seq')
- pred_out: bfloat16 [128, 32, 512], P(('part', 'data'))
- w_enc: bfloat16 [512, 640], replicated
- w_pred: bfloat16 [512, 640], replicated
- w_out: bfloat16 [640, 1024], replicated
- labels: int32 [128, 31], P(('part', 'data'))
- frame_len: int32 [128], P(('part', 'data'))
- label_len: int32 [128], P(('part', 'data'))
Outputs:
- output 1: float32 [128], P(('part', 'data'))
- output 2: bfloat16 [128, 64, 512], P(('part', 'data'), 'seq')
- output 3: float32 [128, 32, 512], P(('part', 'data'))
- output 4: float32 [512, 640], P('part')
- output 5: float32 [512, 640], P('part')
- output 6: float32 [640, 1024], P('part')
All inputs are finite; a program needn't handle non-finite values.
Results may differ from a plain program's by a relative error of at most 0.0127134.
Values are sent between devices in bfloat16 or wider.
A program may use at most 768 MiB of HBM per device.

v0:
```python
import jax
import jax.numpy as jnp
from jax import lax
from jax.sharding import PartitionSpec as P

NEG_FILL = -1e30


def joint_forward(enc_loc, pred_loc, w_enc, w_pred, w_out, lab_ids):
    act_enc = jnp.einsum("bth,hj->btj", enc_loc, w_enc, preferred_element_type=jnp.float32).astype(jnp.bfloat16)
    act_pred = jnp.einsum("buh,hj->buj", pred_loc, w_pred, preferred_element_type=jnp.float32).astype(jnp.bfloat16)
    hidden = jnp.tanh(act_enc.astype(jnp.float32)[:, :, None, :] + act_pred.astype(jnp.float32)[:, None, :, :]).astype(jnp.bfloat16)
    logits = jnp.einsum("btuj,jv->btuv", hidden, w_out, preferred_element_type=jnp.float32)
    log_norm = jax.nn.logsumexp(logits, axis=-1)
    w_label = jnp.take(w_out, lab_ids, axis=1)
    label_logit = jnp.einsum("btuj,jbu->btu", hidden, w_label, preferred_element_type=jnp.float32)
    return hidden, logits, log_norm, logits[..., 0] - log_norm, label_logit - log_norm


def alpha_rows(row_in, blank, lab_cum):
    def frame_step(carry, frame_in):
        blank_t, cum_t = frame_in
        alpha_t = cum_t + lax.cumlogsumexp(carry - cum_t, axis=1)
        return alpha_t + blank_t, alpha_t

    row_out, alpha = lax.scan(frame_step, row_in, (jnp.swapaxes(blank, 0, 1), jnp.swapaxes(lab_cum, 0, 1)))
    return row_out, jnp.swapaxes(alpha, 0, 1)


def beta_rows(row_in, blank, lab_cum, frame_ok, upos_ok, end_row):
    def frame_step(carry, frame_in):
        blank_t, cum_t, valid_t = frame_in
        terms = jnp.where(upos_ok, carry + blank_t + cum_t, NEG_FILL)
        beta_t = jnp.where(upos_ok, lax.cumlogsumexp(terms, axis=1, reverse=True) - cum_t, NEG_FILL)
        beta_t = jnp.where(valid_t[:, None], beta_t, end_row)
        return beta_t, beta_t

    row_out, beta = lax.scan(frame_step, row_in, (jnp.swapaxes(blank, 0, 1), jnp.swapaxes(lab_cum, 0, 1), frame_ok.T), reverse=True)
    return row_out, jnp.swapaxes(beta, 0, 1)


def occupancies(alpha, beta, beta_tail, blank, label_lp, log_prob, frame_ok, label_pos, label_len):
    beta_next = jnp.concatenate([beta[:, 1:], beta_tail[:, None]], axis=1)
    beta_right = jnp.concatenate([beta[:, :, 1:], jnp.full(beta.shape[:2] + (1,), NEG_FILL, jnp.float32)], axis=2)
    shift = log_prob[:, None, None]
    cell_ok = frame_ok[:, :, None] & (label_pos[None, None, :] <= label_len[:, None, None])
    label_ok = cell_ok & (label_pos[None, None, :] < label_len[:, None, None])
    occ_blank = jnp.where(cell_ok, jnp.exp(alpha + blank + beta_next - shift), 0.0)
    occ_label = jnp.where(label_ok, jnp.exp(alpha + label_lp + beta_right - shift), 0.0)
    return occ_blank, occ_label


def joint_backward(enc_loc, hidden, logits, log_norm, lab_ids, occ_blank, occ_label, w_enc, w_out):
    vocab = jnp.arange(w_out.shape[1])
    softmax_p = jnp.exp(logits - log_norm[..., None])
    grad_logits = (softmax_p * (occ_blank + occ_label)[..., None] - jnp.where(vocab == 0, occ_blank[..., None], 0.0) - jnp.where(vocab == lab_ids[:, None, :, None], occ_label[..., None], 0.0)).astype(jnp.bfloat16)
    grad_hidden = jnp.einsum("btuv,jv->btuj", grad_logits, w_out, preferred_element_type=jnp.float32)
    grad_w_out = jnp.einsum("btuj,btuv->jv", hidden, grad_logits, preferred_element_type=jnp.float32)
    grad_pre = grad_hidden * (1.0 - jnp.square(hidden.astype(jnp.float32)))
    grad_act_enc = jnp.sum(grad_pre, axis=2).astype(jnp.bfloat16)
    grad_enc = jnp.einsum("btj,hj->bth", grad_act_enc, w_enc, preferred_element_type=jnp.float32).astype(jnp.bfloat16)
    grad_w_enc = jnp.einsum("bth,btj->hj", enc_loc, grad_act_enc, preferred_element_type=jnp.float32)
    return grad_enc, grad_w_enc, grad_w_out, jnp.sum(grad_pre, axis=1)


def solution(mesh):
    n_seq = mesh.shape["seq"]
    to_right = [(src, src + 1) for src in range(n_seq - 1)]
    to_left = [(src + 1, src) for src in range(n_seq - 1)]
    utt_rows = P(("part", "data"))
    utt_mats = P(("part", "data"), None)
    utt_cube = P(("part", "data"), None, None)
    enc_spec = P(("part", "data"), "seq", None)
    weight_in = P(None, None)
    weight_out = P("part", None)

    def body(enc_loc, pred_loc, w_enc, w_pred, w_out, labels, frame_len, label_len):
        n_utt, t_loc, _ = enc_loc.shape
        n_upos = pred_loc.shape[1]
        seq_pos = lax.axis_index("seq")
        lab_ids = jnp.concatenate([labels, jnp.zeros((n_utt, 1), jnp.int32)], axis=1)
        hidden, logits, log_norm, blank, label_lp = joint_forward(enc_loc, pred_loc, w_enc, w_pred, w_out, lab_ids)
        lab_cum = jnp.concatenate([jnp.zeros((n_utt, t_loc, 1), jnp.float32), jnp.cumsum(label_lp[:, :, :-1], axis=2)], axis=2)
        label_pos = jnp.arange(n_upos)
        frame_pos = seq_pos * t_loc + jnp.arange(t_loc)
        frame_ok = frame_pos[None, :] < frame_len[:, None]
        upos_ok = label_pos[None, :] <= label_len[:, None]
        start_row = jnp.broadcast_to(jnp.where(label_pos == 0, 0.0, NEG_FILL), (n_utt, n_upos)).astype(jnp.float32)
        end_row = jnp.where(label_pos[None, :] == label_len[:, None], 0.0, NEG_FILL).astype(jnp.float32)

        def alpha_hop(hop_idx, row_in):
            row_out, _ = alpha_rows(row_in, blank, lab_cum)
            received = lax.ppermute(row_out, "seq", to_right)
            return jnp.where(seq_pos == 0, start_row, received)

        alpha_in = lax.fori_loop(0, n_seq - 1, alpha_hop, start_row)
        _, alpha = alpha_rows(alpha_in, blank, lab_cum)
        last_cell = (frame_pos[None, :, None] == frame_len[:, None, None] - 1) & (label_pos[None, None, :] == label_len[:, None, None])
        log_prob = lax.psum(jnp.sum(jnp.where(last_cell, alpha + blank, 0.0), axis=(1, 2)), "seq")

        def beta_hop(hop_idx, row_in):
            row_out, _ = beta_rows(row_in, blank, lab_cum, frame_ok, upos_ok, end_row)
            received = lax.ppermute(row_out, "seq", to_left)
            return jnp.where(seq_pos == n_seq - 1, end_row, received)

        beta_in = lax.fori_loop(0, n_seq - 1, beta_hop, end_row)
        _, beta = beta_rows(beta_in, blank, lab_cum, frame_ok, upos_ok, end_row)
        occ_blank, occ_label = occupancies(alpha, beta, beta_in, blank, label_lp, log_prob, frame_ok, label_pos, label_len)
        grad_enc, grad_w_enc, grad_w_out, act_pred_part = joint_backward(enc_loc, hidden, logits, log_norm, lab_ids, occ_blank, occ_label, w_enc, w_out)
        act_pred_grad = lax.psum(act_pred_part, "seq").astype(jnp.bfloat16)
        grad_pred = jnp.einsum("buj,hj->buh", act_pred_grad, w_pred, preferred_element_type=jnp.float32)
        grad_w_pred = jnp.einsum("buh,buj->hj", pred_loc, act_pred_grad, preferred_element_type=jnp.float32)
        grad_w_enc = lax.psum(grad_w_enc, ("data", "seq"))
        grad_w_out = lax.psum(grad_w_out, ("data", "seq"))
        grad_w_pred = lax.psum(grad_w_pred, "data")
        return -log_prob, grad_enc, grad_pred, grad_w_enc, grad_w_pred, grad_w_out

    return jax.shard_map(body, mesh=mesh, in_specs=(enc_spec, utt_cube, weight_in, weight_in, weight_in, utt_mats, utt_rows, utt_rows), out_specs=(utt_rows, enc_spec, utt_cube, weight_out, weight_out, weight_out), check_vma=False)
```

profile of v0, /device:TPU:97, one launch (start us, length us, event | category | flops | bytes accessed | tf_op | source)
XLA Modules:
  0.0 582.2 jit_solution(3785470584593665371)
XLA Ops:
  17.1 8.6 %tanh_convert_fusion = bf16[32,8,32,640]{3,2,1,0:T(8,128)(2,1)} fusion(f32[32,32,640]{2,1,0:T(8,128)} %fusion.33, f32[32,8,640]{2,1,0:T(8,128)S(1)} %fusion.37), kind=kLoop, calls=%fused_computation.44 | loop fusion | flops 10485760 | bytes 13762560 | tf_op jit(solution)/shard_map/convert_element_type | solution.py:12
  25.7 18.9 %fusion.56 = (f32[32,8,32]{2,1,0:T(8,128)S(1)}, f32[32,8,32,1024]{3,2,1,0:T(8,128)}) fusion(bf16[640,1024]{1,0:T(8,128)(2,1)} %param.24, f32[32,32,640]{2,1,0:T(8,128)} %fusion.33, f32[32,8,640]{2,1,0:T(8,128)S(1)} %fusion.37), kind=kOutput, calls=%fused_computation.111 | convolution fusion | flops 10756284416 | bytes 38174720 | tf_op jit(solution)/shard_map/btuj,jv->btuv/dot_general | solution.py:13
  44.7 5.2 gather_fusion
  51.4 11.6 %fusion.25 = f32[32,32,1,8]{3,2,1,0:T(1,128)} fusion(bf16[32,8,32,640]{3,2,1,0:T(8,128)(2,1)} %tanh_convert_fusion, bf16[640,32,32,1]{0,2,1,3:T(8,128)(2,1)S(1)} %select_bitcast_fusion.1), kind=kOutput, calls=%fused_computation.49 | convolution fusion | flops 10485760 | bytes 11829248 | tf_op jit(solution)/shard_map/btuj,jbu->btu/dot_general | solution.py:16
  64.3 13.7 %exponential_reduce_fusion = f32[32,8,32]{2,1,0:T(8,128)S(1)} fusion(f32[32,8,32,1024]{3,2,1,0:T(8,128)} %get-tuple-element.907, f32[32,8,32]{2,1,0:T(8,128)S(1)} %is-finite_select_fusion), kind=kLoop, calls=%fused_computation.42 | loop fusion | flops 16769024 | bytes 33619968 | tf_op jit(solution)/shard_map/reduce_sum | solution.py:14
  78.0 5.9 %reduce_window_sum.11 = f32[32,8,31]{2,1,0:T(8,128)S(1)} reduce-window(f32[32,8,31]{2,1,0:T(8,128)S(1)} %bitcast.206, f32[]{:T(128)} %constant.207.clone.1), window={size=1x1x31 pad=0_0x0_0x30_0}, to_apply=%region_2.3 | reduce-window | flops 238080 | bytes 63492 | tf_op jit(solution)/shard_map/jit(cumsum)/reduce_window_sum | solution.py:83
  87.8 129.1 %while.108 = (s32[]{:T(128)}, f32[32,32]{1,0:T(8,128)S(1)}, pred[]{:T(512)}, f32[32,8,32]{2,0,1:T(8,128)S(1)}, f32[32,8,32]{2,0,1:T(8,128)S(1)}, /*index=5*/s32[...) while((s32[]{:T(128)}, f32[32,32]{1,0:T(8,128)S(1)}, ...), condition=%wide.region_17.18_spmd.clone.clone, body=%wide.region_13.17_spmd.clone.clone.sunk | while | flops 266501 | bytes 73983 | solution.py:106
  88.0 12.9 %while.111 = (s32[]{:T(128)}, f32[32,32]{1,0:T(8,128)S(1)}, pred[8,32]{1,0:T(8,128)(4,1)S(1)}, f32[8,32,32]{2,1,0:T(8,128)S(1)}, f32[8,32,32]{2,1,0:T(8,128)S(1)...) while((s32[]{:T(128)}, f32[32,32]{1,0:T(8,128)S(1)}, ...), condition=%wide.region_16.16_spmd, body=%wide.region_14.15_spmd.sunk | while | flops 260099 | bytes 43233 | solution.py:38
  107.2 12.9 %while.111 = (s32[]{:T(128)}, f32[32,32]{1,0:T(8,128)S(1)}, pred[8,32]{1,0:T(8,128)(4,1)S(1)}, f32[8,32,32]{2,1,0:T(8,128)S(1)}, f32[8,32,32]{2,1,0:T(8,128)S(1)...) while((s32[]{:T(128)}, f32[32,32]{1,0:T(8,128)S(1)}, ...), condition=%wide.region_16.16_spmd, body=%wide.region_14.15_spmd.sunk | while | flops 260099 | bytes 43233 | solution.py:38
  125.6 12.9 %while.111 = (s32[]{:T(128)}, f32[32,32]{1,0:T(8,128)S(1)}, pred[8,32]{1,0:T(8,128)(4,1)S(1)}, f32[8,32,32]{2,1,0:T(8,128)S(1)}, f32[8,32,32]{2,1,0:T(8,128)S(1)...) while((s32[]{:T(128)}, f32[32,32]{1,0:T(8,128)S(1)}, ...), condition=%wide.region_16.16_spmd, body=%wide.region_14.15_spmd.sunk | while | flops 260099 | bytes 43233 | solution.py:38
  143.9 12.9 %while.111 = (s32[]{:T(128)}, f32[32,32]{1,0:T(8,128)S(1)}, pred[8,32]{1,0:T(8,128)(4,1)S(1)}, f32[8,32,32]{2,1,0:T(8,128)S(1)}, f32[8,32,32]{2,1,0:T(8,128)S(1)...) while((s32[]{:T(128)}, f32[32,32]{1,0:T(8,128)S(1)}, ...), condition=%wide.region_16.16_spmd, body=%wide.region_14.15_spmd.sunk | while | flops 260099 | bytes 43233 | solution.py:38
  162.2 12.9 %while.111 = (s32[]{:T(128)}, f32[32,32]{1,0:T(8,128)S(1)}, pred[8,32]{1,0:T(8,128)(4,1)S(1)}, f32[8,32,32]{2,1,0:T(8,128)S(1)}, f32[8,32,32]{2,1,0:T(8,128)S(1)...) while((s32[]{:T(128)}, f32[32,32]{1,0:T(8,128)S(1)}, ...), condition=%wide.region_16.16_spmd, body=%wide.region_14.15_spmd.sunk | while | flops 260099 | bytes 43233 | solution.py:38
  180.5 12.9 %while.111 = (s32[]{:T(128)}, f32[32,32]{1,0:T(8,128)S(1)}, pred[8,32]{1,0:T(8,128)(4,1)S(1)}, f32[8,32,32]{2,1,0:T(8,128)S(1)}, f32[8,32,32]{2,1,0:T(8,128)S(1)...) while((s32[]{:T(128)}, f32[32,32]{1,0:T(8,128)S(1)}, ...), condition=%wide.region_16.16_spmd, body=%wide.region_14.15_spmd.sunk | while | flops 260099 | bytes 43233 | solution.py:38
  198.8 12.9 %while.111 = (s32[]{:T(128)}, f32[32,32]{1,0:T(8,128)S(1)}, pred[8,32]{1,0:T(8,128)(4,1)S(1)}, f32[8,32,32]{2,1,0:T(8,128)S(1)}, f32[8,32,32]{2,1,0:T(8,128)S(1)...) while((s32[]{:T(128)}, f32[32,32]{1,0:T(8,128)S(1)}, ...), condition=%wide.region_16.16_spmd, body=%wide.region_14.15_spmd.sunk | while | flops 260099 | bytes 43233 | solution.py:38
  216.9 14.8 %while.109 = (s32[]{:T(128)}, f32[32,32]{1,0:T(8,128)S(1)}, f32[8,32,32]{2,0,1:T(8,128)S(1)}, pred[8,32]{1,0:T(8,128)(4,1)S(1)}, f32[8,32,32]{2,1,0:T(8,128)S(1)...) while((s32[]{:T(128)}, f32[32,32]{1,0:T(8,128)S(1)}, ...), condition=%wide.region_20.21_spmd.clone.clone, body=%wide.region_18.20_spmd.clone.clone.sunk | while | flops 270339 | bytes 58001 | solution.py:38
  233.6 78.9 %while.106 = (s32[]{:T(128)}, f32[32,32]{1,0:T(8,128)S(1)}, pred[]{:T(512)}, f32[32,8,32]{2,0,1:T(8,128)S(1)}, f32[32,8,32]{2,0,1:T(8,128)S(1)}, /*index=5*/f32[...) while((s32[]{:T(128)}, f32[32,32]{1,0:T(8,128)S(1)}, pred[]{:T(512)}, ...), condition=%wide.region_7.8_spmd.clone, body=%wide.region_3.7_spmd.clone.sunk | while | flops 258052 | bytes 61855 | solution.py:96
  233.6 6.5 %while.110 = (s32[]{:T(128)}, f32[32,32]{1,0:T(8,128)S(1)}, f32[8,32,32]{2,1,0:T(8,128)S(1)}, f32[8,32,32]{2,1,0:T(8,128)S(1)}, s32[]{:T(128)}, /*index=5*/f32[]{:T(128)}) while((s32[]{:T(128)}, f32[32,32]{1,0:T(8,128)S(1)}, f32[8,32,32]{2,1,0:T(8,128)S(1)}, f32[8,32,32]{2,1,0:T(8,128)S(1)}, s32[]{:T(128)}, /*index=5*/f32[]{:T(128)}) %tuple.227), condition=%wide.region_6.6_spmd, body=%wide.region_4.5_spmd.sunk | while | flops 257026 | bytes 36953 | solution.py:26
  243.2 6.5 %while.110 = (s32[]{:T(128)}, f32[32,32]{1,0:T(8,128)S(1)}, f32[8,32,32]{2,1,0:T(8,128)S(1)}, f32[8,32,32]{2,1,0:T(8,128)S(1)}, s32[]{:T(128)}, /*index=5*/f32[]{:T(128)}) while((s32[]{:T(128)}, f32[32,32]{1,0:T(8,128)S(1)}, f32[8,32,32]{2,1,0:T(8,128)S(1)}, f32[8,32,32]{2,1,0:T(8,128)S(1)}, s32[]{:T(128)}, /*index=5*/f32[]{:T(128)}) %tuple.227), condition=%wide.region_6.6_spmd, body=%wide.region_4.5_spmd.sunk | while | flops 257026 | bytes 36953 | solution.py:26
  254.5 6.5 %while.110 = (s32[]{:T(128)}, f32[32,32]{1,0:T(8,128)S(1)}, f32[8,32,32]{2,1,0:T(8,128)S(1)}, f32[8,32,32]{2,1,0:T(8,128)S(1)}, s32[]{:T(128)}, /*index=5*/f32[]{:T(128)}) while((s32[]{:T(128)}, f32[32,32]{1,0:T(8,128)S(1)}, f32[8,32,32]{2,1,0:T(8,128)S(1)}, f32[8,32,32]{2,1,0:T(8,128)S(1)}, s32[]{:T(128)}, /*index=5*/f32[]{:T(128)}) %tuple.227), condition=%wide.region_6.6_spmd, body=%wide.region_4.5_spmd.sunk | while | flops 257026 | bytes 36953 | solution.py:26
  261.0 4.2 collective-permute-start.1
  266.1 6.5 %while.110 = (s32[]{:T(128)}, f32[32,32]{1,0:T(8,128)S(1)}, f32[8,32,32]{2,1,0:T(8,128)S(1)}, f32[8,32,32]{2,1,0:T(8,128)S(1)}, s32[]{:T(128)}, /*index=5*/f32[]{:T(128)}) while((s32[]{:T(128)}, f32[32,32]{1,0:T(8,128)S(1)}, f32[8,32,32]{2,1,0:T(8,128)S(1)}, f32[8,32,32]{2,1,0:T(8,128)S(1)}, s32[]{:T(128)}, /*index=5*/f32[]{:T(128)}) %tuple.227), condition=%wide.region_6.6_spmd, body=%wide.region_4.5_spmd.sunk | while | flops 257026 | bytes 36953 | solution.py:26
  272.6 4.2 collective-permute-start.1
  277.7 6.5 %while.110 = (s32[]{:T(128)}, f32[32,32]{1,0:T(8,128)S(1)}, f32[8,32,32]{2,1,0:T(8,128)S(1)}, f32[8,32,32]{2,1,0:T(8,128)S(1)}, s32[]{:T(128)}, /*index=5*/f32[]{:T(128)}) while((s32[]{:T(128)}, f32[32,32]{1,0:T(8,128)S(1)}, f32[8,32,32]{2,1,0:T(8,128)S(1)}, f32[8,32,32]{2,1,0:T(8,128)S(1)}, s32[]{:T(128)}, /*index=5*/f32[]{:T(128)}) %tuple.227), condition=%wide.region_6.6_spmd, body=%wide.region_4.5_spmd.sunk | while | flops 257026 | bytes 36953 | solution.py:26
  289.3 6.5 %while.110 = (s32[]{:T(128)}, f32[32,32]{1,0:T(8,128)S(1)}, f32[8,32,32]{2,1,0:T(8,128)S(1)}, f32[8,32,32]{2,1,0:T(8,128)S(1)}, s32[]{:T(128)}, /*index=5*/f32[]{:T(128)}) while((s32[]{:T(128)}, f32[32,32]{1,0:T(8,128)S(1)}, f32[8,32,32]{2,1,0:T(8,128)S(1)}, f32[8,32,32]{2,1,0:T(8,128)S(1)}, s32[]{:T(128)}, /*index=5*/f32[]{:T(128)}) %tuple.227), condition=%wide.region_6.6_spmd, body=%wide.region_4.5_spmd.sunk | while | flops 257026 | bytes 36953 | solution.py:26
  300.9 6.5 %while.110 = (s32[]{:T(128)}, f32[32,32]{1,0:T(8,128)S(1)}, f32[8,32,32]{2,1,0:T(8,128)S(1)}, f32[8,32,32]{2,1,0:T(8,128)S(1)}, s32[]{:T(128)}, /*index=5*/f32[]{:T(128)}) while((s32[]{:T(128)}, f32[32,32]{1,0:T(8,128)S(1)}, f32[8,32,32]{2,1,0:T(8,128)S(1)}, f32[8,32,32]{2,1,0:T(8,128)S(1)}, s32[]{:T(128)}, /*index=5*/f32[]{:T(128)}) %tuple.227), condition=%wide.region_6.6_spmd, body=%wide.region_4.5_spmd.sunk | while | flops 257026 | bytes 36953 | solution.py:26
  312.5 7.3 %while.104 = (s32[]{:T(128)}, f32[32,32]{1,0:T(8,128)S(1)}, f32[8,32,32]{2,0,1:T(8,128)S(1)}, f32[8,32,32]{2,1,0:T(8,128)S(1)}, f32[8,32,32]{2,1,0:T(8,128)S(1)}, /*index=5*/s32[]{:T(128)}, f32[]{:T(128)}, s32[]{:T(128)}) while((s32[]{:T(128)}, f32[32,32]{1,0:T(8,128)S(1)}, f32[8,32,32]{2,0,1:T(8,128)S(1)}, f32[8,32,32]{2,1,0:T(8,128)S(1)}, ...), condition=%wide.region_10.11_spmd, body=%wide.region_8.10_spmd.sunk | while | flops 258050 | bytes 57457 | solution.py:26
  320.3 13.4 %psum.35 = f32[32]{0:T(128)S(1)} all-reduce(f32[32]{0:T(128)S(1)} %select_reduce_fusion), channel_id=1, replica_groups=mesh['part'=1,'data'=4,'seq'=8] {'seq'}, use_global_device_ids=true, to_apply=%region_12.13 | all-reduce | flops 32 | bytes 256 | tf_op jit(solution)/shard_map/psum | solution.py:99
  333.8 28.1 %fusion.21 = (f32[32,32,640]{2,1,0:T(8,128)}, bf16[32,8,640]{2,1,0:T(8,128)(2,1)}) fusion(f32[32,32,640]{2,1,0:T(8,128)} %fusion.33, f32[32,8,640]{2,1,0:T(8,128)S(1)} %fusion.37, bf16[640,1024]{1,0:T(8,128)(2,1)} %param.24, f32[32,8,32,1024]{3,2,1,0:T(8,128)} %get-tuple-element.907, f32[32,8,32]{2,1,0:T(8,128)S(1)} %get-tuple-element.896, ...), kind=kOutput, calls=%fused_computation.45 | convolution fusion | flops 10837262336 | bytes 42271744 | tf_op jit(solution)/shard_map/btuv,jv->btuj/dot_general | solution.py:57
  361.9 53.6 %all-reduce.11 = bf16[32,32,640]{2,1,0:T(8,128)(2,1)S(1)} all-reduce(f32[32,32,640]{2,1,0:T(8,128)} %get-tuple-element.816), channel_id=1, replica_groups=mesh['part'=1,'data'=4,'seq'=8] {'seq'}, use_global_device_ids=true, to_apply=%region_23.24 | all-reduce | flops 655360 | bytes 3932160 | tf_op jit(solution)/shard_map/psum | solution.py:110
  417.6 26.6 %fusion.32 = f32[640,1024]{1,0:T(8,128)} fusion(f32[32,32,640]{2,1,0:T(8,128)} %fusion.33, f32[32,8,640]{2,1,0:T(8,128)S(1)} %fusion.37, f32[32,8,32,1024]{3,2,1,0:T(8,128)} %get-tuple-element.907, f32[32,8,32]{2,1,0:T(8,128)} %copy-done.6, f32[32,8,32]{2,1,0:T(8,128)S(1)} %get-tuple-element.895, f32[32,8,32]{2,1,0:T(8,128)S(1)} %get-tuple-element.894, ...), kind=kOutput, calls=%fused_computation.58 | convolution fusion | flops 10806624256 | bytes 40633344 | tf_op jit(solution)/shard_map/btuj,btuv->jv/dot_general | solution.py:58
  450.7 12.0 %all-reduce.8.cloned.1.call-done = f32[512,640]{0,1:T(8,128)} async-done(((f32[512,640]{0,1:T(8,128)}), f32[512,640]{0,1:T(8,128)}) %all-reduce.8.cloned.1.call-update) | async-done | bytes 1310736 | tf_op jit(solution)/shard_map/psum | solution.py:115
  465.5 103.5 %all-reduce.10.cloned.1.call-done = (f32[512,640]{0,1:T(8,128)}, f32[640,1024]{1,0:T(8,128)}) async-done(((f32[512,640]{0,1:T(8,128)}, f32[640,1024]{1,0:T(8,128)}), (f32[512,640]{0,1:T(8,128)}, f32[640,1024]{1,0:T(8,128)})) %all-reduce.10.cloned.1.call-update) | async-done | bytes 3932176 | tf_op jit(solution)/shard_map/psum | solution.py:113
  (605 shorter events, 255.2 us)
Async XLA Ops:
  7.2 6.4 %copy-start = (bf16[32,32,512]{2,1,0:T(8,128)(2,1)S(1)}, bf16[32,32,512]{2,1,0:T(8,128)(2,1)}, u32[]{:S(2)}) copy-start(bf16[32,32,512]{2,1,0:T(8,128)(2,1)} %param.21) | copy-start | bytes 3145732
  7.2 455.6 %all-reduce.8.cloned.1.call-start = ((), (), s32[]{:S(2)}) async-start(), calls=%async_computation | async-start | bytes 2621440 | tf_op jit(solution)/shard_map/psum | solution.py:115
  64.3 23.2 %copy-start.7 = (s32[32]{0:T(128)S(1)}, s32[32]{0:T(128)}, u32[]{:S(2)}) copy-start(s32[32]{0:T(128)} %param.26) | copy-start | bytes 388
  64.3 23.5 %copy-start.2 = (s32[32]{0:T(128)S(1)}, s32[32]{0:T(128)}, u32[]{:S(2)}) copy-start(s32[32]{0:T(128)} %param.27) | copy-start | bytes 388
  100.9 6.0 %collective-permute-start = (f32[32,32]{1,0:T(8,128)S(1)}, f32[32,32]{1,0:T(8,128)S(1)}, u32[]{:S(2)}, u32[]{:S(2)}) collective-permute-start(f32[32,32]{1,0:T(8,128)S(1)} %get-tuple-element.1144), channel_id=1, source_target_pairs={{1,0},{2,1},{3,2},{4,3},{5,4},{6,5},{7,6},{9,8},{10,9},{11,10},{12... | collective-permute-start | bytes 12296 | tf_op jit(solution)/shard_map/while/body/eval_jaxpr/ppermute | solution.py:103
  120.2 5.1 collective-permute-start
  138.5 5.1 collective-permute-start
  156.8 5.1 collective-permute-start
  175.1 5.1 collective-permute-start
  193.4 5.1 collective-permute-start
  211.7 5.1 collective-permute-start
  240.1 3.1 collective-permute-start.1
  249.7 4.8 collective-permute-start.1
  261.0 5.1 collective-permute-start.1
  272.6 5.1 collective-permute-start.1
  284.2 5.1 collective-permute-start.1
  295.8 5.1 collective-permute-start.1
  307.4 5.1 collective-permute-start.1
  333.8 28.1 %copy-start.6 = (f32[32,8,32]{2,1,0:T(8,128)}, f32[32,8,32]{2,1,0:T(8,128)S(1)}, u32[]{:S(2)}) copy-start(f32[32,8,32]{2,1,0:T(8,128)S(1)} %get-tuple-element.896) | copy-start | bytes 98308
  417.5 151.6 %all-reduce.10.cloned.1.call-start = ((), (), s32[]{:S(2)}) async-start(), calls=%async_computation.1 | async-start | bytes 7864320 | tf_op jit(solution)/shard_map/psum | solution.py:113
  417.5 26.6 %copy-start.3 = (bf16[32,8,640]{2,1,0:T(8,128)(2,1)S(1)}, bf16[32,8,640]{2,1,0:T(8,128)(2,1)}, u32[]{:S(2)}) copy-start(bf16[32,8,640]{2,1,0:T(8,128)(2,1)} %get-tuple-element.817) | copy-start | bytes 983044
  417.5 26.6 %copy-start.5 = (bf16[32,8,512]{2,1,0:T(8,128)(2,1)S(1)}, bf16[32,8,512]{2,1,0:T(8,128)(2,1)}, u32[]{:S(2)}) copy-start(bf16[32,8,512]{2,1,0:T(8,128)(2,1)} %param.20) | copy-start | bytes 786436
  444.2 2.0 copy-start.1
  444.2 2.0 copy-start.4
Sparse Core Ops, SparseCore 0:
  417.6 45.1 all-reduce.7
  466.9 102.1 all-reduce.9
where the time goes:
time: 583 us; the launch traced here: 582 us
  other arithmetic  191 us (33%)
  waiting for transfers between devices  143 us (25%)
  matrix products  98.2 us (17%)
  blocking collectives  66.9 us (11%)
  starting transfers between devices  42.8 us (7%)
  local copies, waits for them, and re-layouts  22.9 us (4%)
  between operations  14.4 us (2%)
    psum x1, waiting for transfers between devices, body(): grad_w_enc = lax.psum(grad_w_enc, ('data', 'seq'))  104 us
    another operation x64, other arithmetic, frame_step(): lax.cumlogsumexp(terms, axis=1, reverse=True) - cum_t  96.2 us
    psum x1, blocking collectives, body(): act_pred_grad = lax.psum(act_pred_part, 'seq').astype(jnp.bfloat16)  53.6 us
    another operation x64, other arithmetic, frame_step(): alpha_t = cum_t + lax.cumlogsumexp(carry - cum_t, axis=1)  48.3 us
    dot_general x1, matrix products, joint_backward(): jnp.einsum('btuv,jv->btuj', grad_logits, w_out, preferred_element_type=jn...  28.1 us
    ppermute x7, starting transfers between devices, alpha_hop(): received = lax.ppermute(row_out, 'seq', to_right)  27.1 us
    dot_general x1, matrix products, joint_backward(): jnp.einsum('btuj,btuv->jv', hidden, grad_logits, preferred_element_type=j...  26.6 us
    ppermute x7, waiting for transfers between devices, beta_hop(): received = lax.ppermute(row_out, 'seq', to_left)  20.8 us
  transfers between devices with their start and end apart: 16, of which 16 were waited for; matrix products, arithmetic and copies ran while one was open for 6% of the time, Pallas kernels for 0%

commit v1 on v0

v1 whole, which is shorter than its diff:
```python
import functools

import jax
import jax.numpy as jnp
from jax import lax
from jax.experimental import pallas as pl
from jax.experimental.pallas import tpu as pltpu
from jax.sharding import PartitionSpec as P

NEG = -1e30
MESH = pl.DeviceIdType.MESH
VMEM = pltpu.VMEM
F32 = jnp.float32
BF16 = jnp.bfloat16
VMEM_LIMIT = 67_000_000
SUB = 8
LANES = 128
GROUPS = 8
CORES = 2
RING = 4


def vspec():
    return pl.BlockSpec(memory_space=pltpu.VMEM)


def sspec():
    return pl.BlockSpec(memory_space=pltpu.SMEM)


def exchange_kernel(n_seq, enc_ref, pred_ref, w_enc_ref, w_pred_ref, frames_ref, a_ref, c_ref, send_sem, recv_sem):
    seq = lax.axis_index("seq")
    n_own = frames_ref.shape[1]
    barrier = pltpu.get_barrier_semaphore()
    for hop in range(1, n_seq):
        pl.semaphore_signal(barrier, inc=1, device_id={"seq": lax.rem(seq + hop, n_seq)}, device_id_type=MESH)
    frames_ref[pl.ds(seq, 1)] = enc_ref[pl.ds(seq * n_own, n_own)][None]
    own_pred = pred_ref[pl.ds(seq * n_own, n_own)]
    c_ref[...] = jnp.dot(own_pred.reshape(-1, own_pred.shape[-1]), w_pred_ref[...], preferred_element_type=F32).astype(BF16).astype(F32)
    pl.semaphore_wait(barrier, n_seq - 1)
    copies = []
    for hop in range(1, n_seq):
        peer = lax.rem(seq + hop, n_seq)
        copy = pltpu.make_async_remote_copy(
            src_ref=enc_ref.at[pl.ds(peer * n_own, n_own)],
            dst_ref=frames_ref.at[seq],
            send_sem=send_sem.at[hop - 1],
            recv_sem=recv_sem.at[hop - 1],
            device_id={"seq": peer},
            device_id_type=MESH,
        )
        copy.start()
        copies.append(copy)
    for copy in copies:
        copy.wait()
    frames = frames_ref[...]
    a_ref[...] = jnp.dot(frames.reshape(-1, frames.shape[-1]), w_enc_ref[...], preferred_element_type=F32).astype(BF16).astype(F32)


def exchange(n_seq, enc_loc, pred_loc, w_enc, w_pred):
    n_utt, t_loc, width = enc_loc.shape
    n_own = n_utt // n_seq
    n_upos = pred_loc.shape[1]
    joint = w_enc.shape[1]
    return pl.pallas_call(
        functools.partial(exchange_kernel, n_seq),
        out_shape=(
            jax.ShapeDtypeStruct((n_seq, n_own, t_loc, width), BF16),
            jax.ShapeDtypeStruct((n_seq * n_own * t_loc, joint), F32),
            jax.ShapeDtypeStruct((n_own * n_upos, joint), F32),
        ),
        in_specs=[vspec()] * 4,
        out_specs=(vspec(), vspec(), vspec()),
        scratch_shapes=[pltpu.SemaphoreType.DMA((n_seq - 1,)), pltpu.SemaphoreType.DMA((n_seq - 1,))],
        compiler_params=pltpu.CompilerParams(collective_id=0, has_side_effects=True, vmem_limit_bytes=VMEM_LIMIT),
        name="exchange",
    )(enc_loc, pred_loc, w_enc, w_pred)


def logaddexp(x, y):
    top = jnp.maximum(x, y)
    return top + jnp.log(1.0 + jnp.exp(-jnp.abs(x - y)))


def lattice_kernel(n_own, n_frames, n_upos, seq_ref, flen_ref, llen_ref, labels_ref, a_ref, c_ref, w_ref, wt_ref,
                   da_ref, dc_ref, gw_ref, loss_ref,
                   p_ref, h_ref, blank_ref, label_ref, alpha_ref, beta_ref, ids_ref, dact_ref, dpred_ref):
    vocab = w_ref.shape[1]
    joint = w_ref.shape[0]
    n_vt = vocab // LANES
    rows_g = SUB * SUB
    rows_t = GROUPS * rows_g
    n_diag = n_frames + n_upos - 1
    first = seq_ref[0] * n_own
    lens_t = [flen_ref[first + b] for b in range(n_own)]
    lens_u = [llen_ref[first + b] for b in range(n_own)]
    blocks_t = [lax.div(n + SUB - 1, SUB) for n in lens_t]
    blocks_u = [lax.div(n + SUB, SUB) for n in lens_u]
    starts = [jnp.int32(0)]
    for b in range(n_own):
        starts.append(starts[-1] + blocks_t[b] * blocks_u[b])
    total = starts[-1]
    n_tiles = lax.div(total + GROUPS - 1, GROUPS)

    def decode(n):
        n = jnp.minimum(n, total - 1)
        b = jnp.int32(0)
        base, width = starts[0], blocks_u[0]
        for k in range(1, n_own):
            past = n >= starts[k]
            b = jnp.where(past, k, b)
            base = jnp.where(past, starts[k], base)
            width = jnp.where(past, blocks_u[k], width)
        ti = lax.div(n - base, width)
        return n, b, ti, n - base - ti * width

    pos_col = lax.broadcasted_iota(jnp.int32, (n_upos, n_upos - 1), 0)
    pos_row = lax.broadcasted_iota(jnp.int32, (n_upos, n_upos - 1), 1)
    for b in range(n_own):
        row = labels_ref[pl.ds(first + b, 1), :].astype(F32)
        col = jnp.sum(jnp.where(pos_col == pos_row, row, 0.0), axis=1, keepdims=True)
        ids_ref[pl.ds(b * n_upos, n_upos), :] = jnp.broadcast_to(col, (n_upos, LANES)).astype(jnp.int32)

    blank_ref[...] = jnp.zeros_like(blank_ref)
    label_ref[...] = jnp.zeros_like(label_ref)
    gw_ref[...] = jnp.zeros_like(gw_ref)
    dact_ref[...] = jnp.zeros_like(dact_ref)
    dpred_ref[...] = jnp.zeros_like(dpred_ref)

    lane = lax.broadcasted_iota(jnp.int32, (SUB, LANES), 1)
    vocab_lane = lax.broadcasted_iota(jnp.int32, (rows_t, LANES), 1)

    def tile_ids(groups):
        parts = []
        for _, b, ti, ui in groups:
            ids = ids_ref[pl.ds(pl.multiple_of(b * n_upos + ui * SUB, SUB), SUB), :]
            parts.append(jnp.broadcast_to(ids[None], (SUB, SUB, LANES)).reshape(rows_g, LANES))
        return jnp.concatenate(parts, axis=0)

    def cell_row(ti, k, ui):
        return pl.multiple_of((n_diag - 1 - ti * SUB - k) * n_upos + ui * SUB, SUB)

    def forward(i, carry):
        groups = [decode(i * GROUPS + g) for g in range(GROUPS)]
        parts = []
        for g, (n, b, ti, ui) in enumerate(groups):
            a8 = a_ref[pl.ds(pl.multiple_of((ti * n_own + b) * SUB, SUB), SUB), :]
            c8 = c_ref[pl.ds(pl.multiple_of(b * n_upos + ui * SUB, SUB), SUB), :]
            parts.append(jnp.tanh(a8[:, None, :] + c8[None, :, :]).reshape(rows_g, joint).astype(BF16))
        h = jnp.concatenate(parts, axis=0)
        row0 = pl.multiple_of(i * rows_t, rows_t)
        h_ref[pl.ds(row0, rows_t), :] = h
        z = jnp.dot(h, w_ref[...], preferred_element_type=F32)
        top = jnp.max(z, axis=1, keepdims=True)
        e = jnp.exp(z - top)
        norm = jnp.sum(e, axis=1, keepdims=True)
        p_ref[pl.ds(row0, rows_t), :] = e * (1.0 / norm)
        log_norm = top + jnp.log(norm)
        ids = tile_ids(groups)
        picked = jnp.zeros((rows_t, LANES), F32)
        for v in range(n_vt):
            picked = picked + jnp.where(vocab_lane + v * LANES == ids, z[:, v * LANES:(v + 1) * LANES], 0.0)
        label = jnp.sum(picked, axis=1, keepdims=True) - log_norm
        blank = z[:, 0:1] - log_norm
        for g, (n, b, ti, ui) in enumerate(groups):
            for k in range(SUB):
                at = cell_row(ti, k, ui)
                lo = g * rows_g + k * SUB
                blank_ref[pl.ds(at, SUB), :] = jnp.where(lane == b, blank[lo:lo + SUB], blank_ref[pl.ds(at, SUB), :])
                label_ref[pl.ds(at, SUB), :] = jnp.where(lane == b, label[lo:lo + SUB], label_ref[pl.ds(at, SUB), :])
        return carry

    lax.fori_loop(0, n_tiles, forward, 0)

    upos = lax.broadcasted_iota(jnp.int32, (n_upos, LANES), 0)
    utt = lax.broadcasted_iota(jnp.int32, (n_upos, LANES), 1)
    t_end = jnp.ones((n_upos, LANES), jnp.int32)
    u_end = jnp.zeros((n_upos, LANES), jnp.int32)
    for b in range(n_own):
        t_end = jnp.where(utt == b, lens_t[b], t_end)
        u_end = jnp.where(utt == b, lens_u[b], u_end)

    def diagonal(d):
        return pl.ds((n_diag - 1 - d) * n_upos, n_upos, stride=n_upos + 1)

    def down(x):
        return jnp.where(upos == 0, NEG, pltpu.roll(x, 1, 0))

    def up(x):
        return jnp.where(upos == n_upos - 1, NEG, pltpu.roll(x, n_upos - 1, 0))

    def edge(d):
        return jnp.where((d - upos == t_end) & (upos == u_end), 0.0, NEG)

    alpha0 = jnp.where(upos == 0, 0.0, NEG).astype(F32)
    beta0 = edge(n_diag)
    alpha_ref[0] = alpha0
    beta_ref[n_diag] = beta0

    def sweep(k, carry):
        alpha, beta = carry
        d = k + 1
        alpha = logaddexp(alpha + blank_ref[diagonal(k), :], down(alpha + label_ref[diagonal(k), :]))
        alpha = jnp.where(upos <= d, alpha, NEG)
        alpha_ref[d] = alpha
        d = n_diag - 1 - k
        inside = (d - upos < t_end) & (upos <= u_end)
        beta = logaddexp(beta + blank_ref[diagonal(d), :], up(beta) + label_ref[diagonal(d), :])
        beta = jnp.where(inside, beta, edge(d))
        beta_ref[d] = beta
        return alpha, beta

    lax.fori_loop(0, n_diag, sweep, (alpha0, beta0))
    log_prob = beta_ref[0][0:1, :]
    loss_ref[...] = jnp.broadcast_to(-log_prob, (SUB, LANES))

    def occupancy(d, carry):
        t = d - upos
        alpha = alpha_ref[d]
        after = beta_ref[d + 1]
        cell_ok = (t >= 0) & (t < t_end) & (upos <= u_end)
        q0 = jnp.where(cell_ok, jnp.exp(alpha + blank_ref[diagonal(d), :] + after - log_prob), 0.0)
        q1 = jnp.where(cell_ok & (upos < u_end), jnp.exp(alpha + label_ref[diagonal(d), :] + up(after) - log_prob), 0.0)
        blank_ref[diagonal(d), :] = q0
        label_ref[diagonal(d), :] = q1
        return carry

    lax.fori_loop(0, n_diag, occupancy, 0)

    def backward(i, carry):
        groups = [decode(i * GROUPS + g) for g in range(GROUPS)]
        row0 = pl.multiple_of(i * rows_t, rows_t)
        q0s, q1s = [], []
        for g, (n, b, ti, ui) in enumerate(groups):
            keep = (lane == b) & (i * GROUPS + g < total)
            for k in range(SUB):
                at = cell_row(ti, k, ui)
                q0s.append(jnp.where(keep, blank_ref[pl.ds(at, SUB), :], 0.0))
                q1s.append(jnp.where(keep, label_ref[pl.ds(at, SUB), :], 0.0))
        q0 = jnp.sum(jnp.concatenate(q0s, axis=0), axis=1, keepdims=True)
        q1 = jnp.sum(jnp.concatenate(q1s, axis=0), axis=1, keepdims=True)
        both = q0 + q1
        ids = tile_ids(groups)
        cols = []
        for v in range(n_vt):
            at_v = vocab_lane + v * LANES
            dz = p_ref[pl.ds(row0, rows_t), v * LANES:(v + 1) * LANES] * both
            if v == 0:
                dz = dz - jnp.where(at_v == 0, q0, 0.0)
            dz = dz - jnp.where(at_v == ids, q1, 0.0)
            cols.append(dz.astype(BF16))
        dz = jnp.concatenate(cols, axis=1)
        h = h_ref[pl.ds(row0, rows_t), :]
        dh = jnp.dot(dz, wt_ref[...], preferred_element_type=F32)
        hf = h.astype(F32)
        ds = dh * (1.0 - hf * hf)
        for g, (n, b, ti, ui) in enumerate(groups):
            cube = ds[g * rows_g:(g + 1) * rows_g].reshape(SUB, SUB, joint)
            at = pl.multiple_of((ti * n_own + b) * SUB, SUB)
            dact_ref[pl.ds(at, SUB), :] += jnp.sum(cube, axis=1)
            at = pl.multiple_of(b * n_upos + ui * SUB, SUB)
            dpred_ref[pl.ds(at, SUB), :] += jnp.sum(cube, axis=0)
        for y in range(gw_ref.shape[0]):
            part = dz[:, y * gw_ref.shape[2]:(y + 1) * gw_ref.shape[2]]
            gw_ref[y] += lax.dot_general(h, part, (((0,), (0,)), ((), ())), preferred_element_type=F32)
        return carry

    lax.fori_loop(0, n_tiles, backward, 0)
    da_ref[...] = dact_ref[...].astype(BF16)
    dc_ref[...] = dpred_ref[...].astype(BF16)


def lattice(n_seq, n_data, seq_idx, frame_len, label_len, labels, act, pred, w_out, w_out_t, n_upos, t_loc):
    n_own = frame_len.shape[0] // n_seq
    n_frames = n_seq * t_loc
    joint, vocab = w_out.shape
    cells = n_own * n_frames * n_upos
    n_diag = n_frames + n_upos - 1
    lat_rows = (n_diag + n_upos - 1) * n_upos
    return pl.pallas_call(
        functools.partial(lattice_kernel, n_own, n_frames, n_upos),
        out_shape=(
            jax.ShapeDtypeStruct(act.shape, BF16),
            jax.ShapeDtypeStruct(pred.shape, BF16),
            jax.ShapeDtypeStruct((n_data, joint, vocab // n_data), F32),
            jax.ShapeDtypeStruct((SUB, LANES), F32),
        ),
        in_specs=[sspec(), sspec(), sspec()] + [vspec()] * 5,
        out_specs=(vspec(),) * 4,
        scratch_shapes=[
            VMEM((cells, vocab), F32),
            VMEM((cells, joint), BF16),
            VMEM((lat_rows, LANES), F32),
            VMEM((lat_rows, LANES), F32),
            VMEM((n_diag + 1, n_upos, LANES), F32),
            VMEM((n_diag + 1, n_upos, LANES), F32),
            VMEM((n_own * n_upos, LANES), jnp.int32),
            VMEM(act.shape, F32),
            VMEM(pred.shape, F32),
        ],
        compiler_params=pltpu.CompilerParams(vmem_limit_bytes=VMEM_LIMIT),
        name="lattice",
    )(seq_idx, frame_len, label_len, labels, act, pred, w_out, w_out_t)


class Copies:
    def __init__(self, send_sem, recv_sem):
        self.sems = (send_sem, recv_sem)
        self.all = []

    def start(self, src, dst, device):
        k = len(self.all)
        copy = pltpu.make_async_remote_copy(src_ref=src, dst_ref=dst, send_sem=self.sems[0].at[k], recv_sem=self.sems[1].at[k], device_id=device, device_id_type=MESH)
        copy.start()
        self.all.append(copy)
        return copy

    def drain(self):
        for copy in self.all:
            copy.wait_send()


class Reduce:
    def __init__(self, copies, axis, me, acc, pair, left, right):
        self.copies, self.acc, self.pair, self.left, self.right = copies, acc, pair, left, right
        self.me, self.nxt, self.prv, self.opp = me, lax.rem(me + 1, RING), lax.rem(me + RING - 1, RING), lax.rem(me + 2, RING)
        self.to_right = {axis: self.nxt}
        self.to_left = {axis: self.prv}

    def begin(self, right_dev, left_dev):
        c, acc = self.copies, self.acc
        self.devs = (right_dev, left_dev)
        self.a1 = c.start(acc(self.opp, 0), self.pair(0), right_dev)
        self.b1 = c.start(acc(self.opp, 1), self.pair(1), left_dev)
        self.b2 = c.start(acc(self.nxt, 1), self.left(1), right_dev)
        self.a2 = c.start(acc(self.prv, 0), self.right(0), left_dev)

    def middle(self):
        c, acc = self.copies, self.acc
        self.a1.wait_recv()
        add = acc(self.nxt, 0)
        add[...] = add[...] + self.pair(0)[...]
        self.a3 = c.start(add, self.left(0), self.devs[0])
        self.b1.wait_recv()
        add = acc(self.prv, 1)
        add[...] = add[...] + self.pair(1)[...]
        self.b3 = c.start(add, self.right(1), self.devs[1])

    def end(self, store):
        self.b2.wait_recv()
        self.a3.wait_recv()
        self.a2.wait_recv()
        self.b3.wait_recv()
        for half in range(2):
            store(half, self.acc(self.me, half)[...] + self.left(half)[...] + self.right(half)[...])


class Gather:
    def __init__(self, copies, me, out, right_dev, left_dev):
        self.copies, self.out, self.devs = copies, out, (right_dev, left_dev)
        self.me, self.nxt, self.prv, self.opp = me, lax.rem(me + 1, RING), lax.rem(me + RING - 1, RING), lax.rem(me + 2, RING)

    def begin(self):
        c, out, (right_dev, left_dev) = self.copies, self.out, self.devs
        self.ra = c.start(out(self.me, 0), out(self.me, 0), right_dev)
        self.lb = c.start(out(self.me, 1), out(self.me, 1), left_dev)
        self.rb = c.start(out(self.me, 1), out(self.me, 1), right_dev)
        self.la = c.start(out(self.me, 0), out(self.me, 0), left_dev)

    def relay(self):
        c, out, (right_dev, left_dev) = self.copies, self.out, self.devs
        self.ra.wait_recv()
        self.ra2 = c.start(out(self.prv, 0), out(self.prv, 0), right_dev)
        self.lb.wait_recv()
        self.lb2 = c.start(out(self.nxt, 1), out(self.nxt, 1), left_dev)
        self.rb.wait_recv()
        self.la.wait_recv()

    def finish(self):
        self.ra2.wait_recv()
        self.lb2.wait_recv()


def combine_kernel(n_seq, n_data, frames_ref, pred_ref, da_ref, dc_ref, gw_ref, loss_ref,
                   da_out, dc_out, gj_out, gw_out, loss_out,
                   gj_acc, gw_acc, gj_pair, gw_pair, gj_py, gj_ly, gj_ry, gj_px, gj_lx, gj_rx, gw_px, gw_lx, gw_rx, gw_py, gw_ly, gw_ry, gj_mid, gw_mid,
                   send_sem, recv_sem):
    seq = lax.axis_index("seq")
    y = lax.axis_index("data")
    x = lax.div(seq, CORES)
    core = lax.rem(seq, CORES)
    n_own = frames_ref.shape[1]
    x_right = {"seq": lax.rem(x + 1, RING) * CORES + core}
    x_left = {"seq": lax.rem(x + RING - 1, RING) * CORES + core}
    y_right = {"data": lax.rem(y + 1, RING)}
    y_left = {"data": lax.rem(y + RING - 1, RING)}
    mate = {"seq": x * CORES + 1 - core}
    barrier = pltpu.get_barrier_semaphore()
    for hop in range(1, n_seq):
        pl.semaphore_signal(barrier, inc=1, device_id={"seq": lax.rem(seq + hop, n_seq)}, device_id_type=MESH)
    for dev in (y_right, y_left):
        pl.semaphore_signal(barrier, inc=1, device_id=dev, device_id_type=MESH)

    frames = frames_ref[...]
    contract_rows = (((0,), (0,)), ((), ()))
    gj_acc[0] = lax.dot_general(frames.reshape(-1, frames.shape[-1]), da_ref[...].reshape(-1, da_ref.shape[-1]), contract_rows, preferred_element_type=F32)
    own_pred = pred_ref[pl.ds(seq * n_own, n_own)]
    gj_acc[1] = lax.dot_general(own_pred.reshape(-1, own_pred.shape[-1]), dc_ref[...], contract_rows, preferred_element_type=F32)
    da_out[pl.ds(seq, 1)] = da_ref[pl.ds(seq, 1)]
    dc_out[pl.ds(seq, 1)] = dc_ref[...][None]
    loss_out[pl.ds(seq, 1)] = loss_ref[...][None]
    pl.semaphore_wait(barrier, n_seq - 1 + 2)

    copies = Copies(send_sem, recv_sem)
    gj_half = gj_acc.shape[1] // CORES
    gw_half = gw_ref.shape[1] // CORES
    gj_y, gw_x = gj_half // RING, gw_half // RING
    gj_x = gj_y // RING

    mate_gj = copies.start(gj_acc.at[:, pl.ds((1 - core) * gj_half, gj_half), :], gj_pair, mate)
    mate_gw = copies.start(gw_ref.at[:, pl.ds((1 - core) * gw_half, gw_half), :], gw_pair, mate)

    dc_half = dc_out.shape[1] // 2

    def dc_at(k, half):
        return dc_out.at[k * CORES + core, pl.ds(half * dc_half, dc_half), :]

    dc_gather = Gather(copies, x, dc_at, x_right, x_left)
    dc_gather.begin()
    dc_mate = [copies.start(dc_out.at[seq], dc_out.at[seq], mate)]
    small = []
    for hop in range(1, n_seq):
        peer = lax.rem(seq + hop, n_seq)
        small.append(copies.start(da_ref.at[peer], da_out.at[seq], {"seq": peer}))
        small.append(copies.start(loss_ref, loss_out.at[seq], {"seq": peer}))

    gj_row = pl.multiple_of(core * gj_half, gj_half)
    gw_row = pl.multiple_of(core * gw_half, gw_half)

    def gj_shard_y(k, half):
        return gj_acc.at[:, pl.ds(pl.multiple_of(gj_row + k * gj_y + half * (gj_y // 2), SUB), gj_y // 2), :]

    def gw_shard_x(k, half):
        return gw_acc.at[:, pl.ds(pl.multiple_of(k * gw_x + half * (gw_x // 2), SUB), gw_x // 2), :]

    def halves(ref):
        return lambda half: ref.at[half]

    mate_gj.wait_recv()
    gj_acc[:, pl.ds(gj_row, gj_half), :] = gj_acc[:, pl.ds(gj_row, gj_half), :] + gj_pair[...]
    gj_r1 = Reduce(copies, "data", y, gj_shard_y, halves(gj_py), halves(gj_ly), halves(gj_ry))
    gj_r1.begin(y_right, y_left)
    mate_gw.wait_recv()
    gw_acc[...] = gw_ref[:, pl.ds(gw_row, gw_half), :] + gw_pair[...]
    gw_r1 = Reduce(copies, "seq", x, gw_shard_x, halves(gw_px), halves(gw_lx), halves(gw_rx))
    gw_r1.begin(x_right, x_left)

    dc_gather.relay()
    dc_mate.append(copies.start(dc_out.at[dc_gather.prv * CORES + core], dc_out.at[dc_gather.prv * CORES + core], mate))
    dc_mate.append(copies.start(dc_out.at[dc_gather.nxt * CORES + core], dc_out.at[dc_gather.nxt * CORES + core], mate))
    gj_r1.middle()
    gw_r1.middle()

    def keep_gj(half, value):
        gj_mid[:, pl.ds(half * (gj_y // 2), gj_y // 2), :] = value

    gj_r1.end(keep_gj)

    def gj_shard_x(k, half):
        return gj_mid.at[:, pl.ds(pl.multiple_of(k * gj_x + half * (gj_x // 2), SUB), gj_x // 2), :]

    gj_r2 = Reduce(copies, "seq", x, gj_shard_x, halves(gj_px), halves(gj_lx), halves(gj_rx))
    gj_r2.begin(x_right, x_left)

    def keep_gw(half, value):
        gw_mid[:, pl.ds(half * (gw_x // 2), gw_x // 2), :] = value

    gw_r1.end(keep_gw)

    def gw_shard_y(k, half):
        return gw_mid.at[k, pl.ds(half * (gw_x // 2), gw_x // 2), :]

    gw_r2 = Reduce(copies, "data", y, gw_shard_y, halves(gw_py), halves(gw_ly), halves(gw_ry))
    gw_r2.begin(y_right, y_left)
    gj_r2.middle()
    gw_r2.middle()

    def gj_out_x(k, half):
        return gj_out.at[:, pl.ds(pl.multiple_of(gj_row + y * gj_y + k * gj_x + half * (gj_x // 2), SUB), gj_x // 2), :]

    def gw_out_y(k, half):
        return gw_out.at[k, pl.ds(pl.multiple_of(gw_row + x * gw_x + half * (gw_x // 2), SUB), gw_x // 2), :]

    def put_gj(half, value):
        gj_out_x(x, half)[...] = value

    def put_gw(half, value):
        gw_out_y(y, half)[...] = value

    gj_r2.end(put_gj)
    gj_g1 = Gather(copies, x, gj_out_x, x_right, x_left)
    gj_g1.begin()
    gw_r2.end(put_gw)
    gw_g1 = Gather(copies, y, gw_out_y, y_right, y_left)
    gw_g1.begin()
    gj_g1.relay()
    gw_g1.relay()
    gj_g1.finish()

    def gj_out_y(k, half):
        return gj_out.at[:, pl.ds(pl.multiple_of(gj_row + k * gj_y + half * (gj_y // 2), SUB), gj_y // 2), :]

    def gw_out_x(k, half):
        return gw_out.at[:, pl.ds(pl.multiple_of(gw_row + k * gw_x + half * (gw_x // 2), SUB), gw_x // 2), :]

    gj_g2 = Gather(copies, y, gj_out_y, y_right, y_left)
    gj_g2.begin()
    gw_g1.finish()
    gw_g2 = Gather(copies, x, gw_out_x, x_right, x_left)
    gw_g2.begin()

    def gj_whole(k):
        return gj_out.at[:, pl.ds(pl.multiple_of(gj_row + k * gj_y, SUB), gj_y), :]

    def gw_whole(k):
        return gw_out.at[:, pl.ds(pl.multiple_of(gw_row + k * gw_x, SUB), gw_x), :]

    last = [copies.start(gj_whole(y), gj_whole(y), mate), copies.start(gw_whole(x), gw_whole(x), mate)]
    dc_gather.finish()
    dc_mate.append(copies.start(dc_out.at[dc_gather.opp * CORES + core], dc_out.at[dc_gather.opp * CORES + core], mate))
    gj_g2.relay()
    for k in (gj_g2.prv, gj_g2.nxt):
        last.append(copies.start(gj_whole(k), gj_whole(k), mate))
    gw_g2.relay()
    for k in (gw_g2.prv, gw_g2.nxt):
        last.append(copies.start(gw_whole(k), gw_whole(k), mate))
    gj_g2.finish()
    last.append(copies.start(gj_whole(gj_g2.opp), gj_whole(gj_g2.opp), mate))
    gw_g2.finish()
    last.append(copies.start(gw_whole(gw_g2.opp), gw_whole(gw_g2.opp), mate))
    for copy in small + dc_mate + last:
        copy.wait_recv()
    copies.drain()


N_COPIES = 6 + 2 + 4 + 14 + 4 * 6 + 4 * 6 + 8


def combine(n_seq, n_data, frames, pred_loc, da, dc, gw, loss):
    _, n_own, t_loc, width = frames.shape
    joint = da.shape[-1]
    n_cols, _, col = gw.shape
    gj_half, gw_half = width // CORES, joint // CORES
    gj_y, gw_x = gj_half // RING, gw_half // RING
    gj_x = gj_y // RING
    return pl.pallas_call(
        functools.partial(combine_kernel, n_seq, n_data),
        out_shape=(
            jax.ShapeDtypeStruct((n_seq, n_own, t_loc, joint), BF16),
            jax.ShapeDtypeStruct((n_seq,) + dc.shape, BF16),
            jax.ShapeDtypeStruct((2, width, joint), F32),
            jax.ShapeDtypeStruct(gw.shape, F32),
            jax.ShapeDtypeStruct((n_seq,) + loss.shape, F32),
        ),
        in_specs=[vspec()] * 6,
        out_specs=(vspec(),) * 5,
        scratch_shapes=[
            VMEM((2, width, joint), F32),
            VMEM((n_cols, gw_half, col), F32),
            VMEM((2, gj_half, joint), F32),
            VMEM((n_cols, gw_half, col), F32),
        ]
        + [VMEM((2, 2, gj_y // 2, joint), F32)] * 3
        + [VMEM((2, 2, gj_x // 2, joint), F32)] * 3
        + [VMEM((2, n_cols, gw_x // 2, col), F32)] * 3
        + [VMEM((2, gw_x // 2, col), F32)] * 3
        + [
            VMEM((2, gj_y, joint), F32),
            VMEM((n_cols, gw_x, col), F32),
            pltpu.SemaphoreType.DMA((N_COPIES,)),
            pltpu.SemaphoreType.DMA((N_COPIES,)),
        ],
        compiler_params=pltpu.CompilerParams(collective_id=1, has_side_effects=True, vmem_limit_bytes=VMEM_LIMIT),
        name="combine",
    )(frames, pred_loc, da.reshape(n_seq, n_own, t_loc, joint), dc, gw, loss)


def solution(mesh):
    n_seq = mesh.shape["seq"]
    n_data = mesh.shape["data"]
    utt_rows = P(("part", "data"))
    utt_mats = P(("part", "data"), None)
    utt_cube = P(("part", "data"), None, None)
    enc_spec = P(("part", "data"), "seq", None)
    weight_in = P(None, None)
    weight_out = P("part", None)

    def body(enc_loc, pred_loc, w_enc, w_pred, w_out, labels, frame_len, label_len):
        n_utt, t_loc, width = enc_loc.shape
        n_own = n_utt // n_seq
        n_upos = pred_loc.shape[1]
        joint, vocab = w_out.shape
        seq_idx = lax.axis_index("seq").astype(jnp.int32).reshape(1)
        frames, act, pred = exchange(n_seq, enc_loc, pred_loc, w_enc, w_pred)
        da, dc, gw, loss = lattice(n_seq, n_data, seq_idx, frame_len, label_len, labels, act, pred, w_out, w_out.T, n_upos, t_loc)
        da_loc, dc_all, gj, gw, loss_all = combine(n_seq, n_data, frames, pred_loc, da, dc, gw, loss)
        grad_enc = jnp.einsum("btj,hj->bth", da_loc.reshape(n_utt, t_loc, joint), w_enc, preferred_element_type=F32).astype(BF16)
        grad_pred = jnp.einsum("buj,hj->buh", dc_all.reshape(n_utt, n_upos, joint), w_pred, preferred_element_type=F32)
        grad_w_out = jnp.swapaxes(gw, 0, 1).reshape(joint, vocab)
        return loss_all[:, 0, :n_own].reshape(n_utt), grad_enc, grad_pred, gj[0], gj[1], grad_w_out

    return jax.shard_map(body, mesh=mesh, in_specs=(enc_spec, utt_cube, weight_in, weight_in, weight_in, utt_mats, utt_rows, utt_rows), out_specs=(utt_rows, enc_spec, utt_cube, weight_out, weight_out, weight_out), check_vma=False)
```

time: 583 us -> 145 us (0.25)
  other arithmetic: 191 us -> 0 us
  waiting for transfers between devices: 143 us -> 0 us
  Pallas kernels: 0 us -> 127 us
  matrix products: 98.2 us -> 5.94 us
  blocking collectives: 66.9 us -> 0 us
  starting transfers between devices: 42.8 us -> 0 us
  between operations: 14.4 us -> 0.67 us
  local copies, waits for them, and re-layouts: 22.9 us -> 11.5 us
    another operation x129 -> x0, other arithmetic: 150 us -> none  [the longest x64 96.2 us: frame_step(): lax.cumlogsumexp(terms, axis=1, reverse=True) - cum_t]
    pallas_call x0 -> x3, Pallas kernels: none -> 127 us  [the longest x1 77.4 us: combine(): pl.pallas_call(functools.partial(combine_kernel, n_seq, n_data), out_shap...]
    psum x2 -> x0, waiting for transfers between devices: 116 us -> none  [the longest x1 104 us: body(): grad_w_enc = lax.psum(grad_w_enc, ('data', 'seq'))]
    dot_general x10 -> x2, matrix products: 98.2 us -> 5.94 us  [the longest x1 3.64 us: body(): jnp.einsum('buj,hj->buh', dc_all.reshape(n_utt, n_upos, joint), w_pred, p...]
    psum x2 -> x0, blocking collectives: 66.9 us -> none  [the longest x1 53.6 us: body(): act_pred_grad = lax.psum(act_pred_part, 'seq').astype(jnp.bfloat16)]
    ppermute x14 -> x0, starting transfers between devices: 42.7 us -> none  [the longest x7 27.1 us: alpha_hop(): received = lax.ppermute(row_out, 'seq', to_right)]
    ppermute x14 -> x0, waiting for transfers between devices: 27 us -> none  [the longest x7 20.8 us: beta_hop(): received = lax.ppermute(row_out, 'seq', to_left)]
    reduce_sum x2 -> x0, other arithmetic: 14.2 us -> none  [the longest x1 13.7 us: joint_forward(): log_norm = jax.nn.logsumexp(logits, axis=-1)]
  transfers between devices with their start and end apart: 16 -> 0, of which waited for: 16 -> 0; matrix products, arithmetic and copies ran while one was open for 6% -> 0% of each run, Pallas kernels for 0% -> 0%
where the time goes in v1:
time: 145 us
  Pallas kernels  127 us (88%)
  local copies, waits for them, and re-layouts  11.5 us (8%)
  matrix products  5.94 us (4%)
    pallas_call x1, Pallas kernels, combine(): pl.pallas_call(functools.partial(combine_kernel, n_seq, n_data), out_shap...  77.4 us
    pallas_call x1, Pallas kernels, lattice(): pl.pallas_call(functools.partial(lattice_kernel, n_own, n_frames, n_upos)...  37.1 us
    pallas_call x1, Pallas kernels, exchange(): pl.pallas_call(functools.partial(exchange_kernel, n_seq), out_shape=(jax....  12.4 us
    unnamed x4, local copies, waits for them, and re-layouts  4.52 us
    dot_general x1, matrix products, body(): jnp.einsum('buj,hj->buh', dc_all.reshape(n_utt, n_upos, joint), w_pred, p...  3.64 us
    squeeze x1, local copies, waits for them, and re-layouts, body(): gj[1]  3.37 us

profile of v1, /device:TPU:97, one launch (start us, length us, event | category | flops | bytes accessed | tf_op | source)
XLA Modules:
  0.0 145.1 jit_solution(7413627065307811708)
XLA Ops:
  0.6 12.4 %exchange.1 = (bf16[8,4,8,512]{3,2,1,0:T(8,128)(2,1)}, f32[256,640]{1,0:T(8,128)}, f32[128,640]{1,0:T(8,128)}) custom-call(bf16[32,8,512]{2,1,0:T(8,128)(2,1)} %enc_ref.1, bf16[32,32,512]{2,1,0:T(8,128)(2,1)} %pred_ref.3, bf16[512,640]{1,0:T(8,128)(2,1)} %w_enc_ref.1, bf16[512,640]{1,0:T(8,128)(2,1)} %w_pred_ref.1), custom_call_target="tpu_custom_call" | custom-call | tf_op jit(solution)/shard_map/exchange/pallas_call | solution.py:65
  13.1 2.4 %copy.15 = bf16[640,1024]{0,1:T(8,128)(2,1)} copy(bf16[640,1024]{1,0:T(8,128)(2,1)} %w_ref.1) | data formatting | bytes 2621440 | tf_op args[4]
  15.5 37.1 %lattice.1 = (bf16[256,640]{1,0:T(8,128)(2,1)}, bf16[128,640]{1,0:T(8,128)(2,1)}, f32[4,640,256]{2,1,0:T(8,128)}, f32[8,128]{1,0:T(8,128)}) custom-call(s32[1]{0:T(128)} %bitcast.seq_ref, s32[32]{0:T(128)} %flen_ref.1, s32[32]{0:T(128)} %llen_ref.1, s32[32,31]{1,0:T(8,128)} %labels_ref.1, f32[256,640]{1,0:T(8,128)} %get-tuple-element.19.a_ref, ...), custom_call_target="tpu_custom_call" | custom-call | tf_op jit(solution)/shard_map/lattice/pallas_call | solution.py:280
  52.6 77.4 %combine.1 = (bf16[8,4,8,640]{3,2,1,0:T(8,128)(2,1)}, bf16[8,128,640]{2,1,0:T(8,128)(2,1)}, f32[2,512,640]{2,1,0:T(8,128)}, f32[4,640,256]{2,1,0:T(8,128)}, f32[8,8,128]{2,1,0:T(8,128)}) custom-call(bf16[8,4,8,512]{3,2,1,0:T(8,128)(2,1)} %get-tuple-element.18.frames_ref, bf16[32,32,512]{2,1,0:T(8,128)(2,1)} %pred_ref.3, bf16[8,4,8,640]{3,2,1,0:T(8,128)(2,1)} %bitcast.23, ...), custom_call_target="tpu_custom_call" | custom-call | tf_op jit(solution)/shard_map/combine/pallas_call | solution.py:556
  130.1 0.0 copy-start
  130.1 0.8 slice_reduce_fusion
  130.9 0.6 reshape_squeeze.3
  131.5 2.3 %convolution_convert_fusion = bf16[32,8,512]{2,1,0:T(8,128)(2,1)} fusion(bf16[32,8,640]{2,1,0:T(8,128)(2,1)} %bitcast.24, bf16[512,640]{1,0:T(8,128)(2,1)} %w_enc_ref.1), kind=kOutput, calls=%fused_computation.2 | convolution fusion | flops 167903232 | bytes 1245184 | tf_op jit(solution)/shard_map/btj,hj->bth/dot_general | solution.py:607
  133.8 0.0 copy-done
  133.8 3.6 %fusion = f32[32,32,512]{2,1,0:T(8,128)} fusion(bf16[32,32,640]{2,1,0:T(8,128)(2,1)} %bitcast.22, bf16[512,640]{1,0:T(8,128)(2,1)S(1)} %copy-done), kind=kOutput, calls=%fused_computation.3 | convolution fusion | flops 671088640 | bytes 4063232 | tf_op jit(solution)/shard_map/buj,hj->buh/dot_general | solution.py:608
  137.5 2.1 %copy.16 = f32[640,4,256]{0,2,1:T(8,128)S(1)} copy(f32[640,4,256]{2,0,1:T(8,128)} %bitcast.21) | data formatting | bytes 5242880 | tf_op jit(solution)/shard_map/transpose | solution.py:609
  139.6 2.1 %copy.17 = f32[640,1024]{1,0:T(8,128)} copy(f32[640,1024]{0,1:T(8,128)S(1)} %bitcast.19) | data formatting | bytes 5242880
  141.7 3.4 %slice_bitcast_fusion = (f32[512,640]{1,0:T(8,128)}, f32[512,640]{1,0:T(8,128)}) fusion(f32[2,512,640]{2,1,0:T(8,128)} %get-tuple-element.28), kind=kLoop, calls=%fused_computation | loop fusion | bytes 5242880 | tf_op jit(solution)/shard_map/squeeze | solution.py:610
Async XLA Ops:
  130.1 3.7 %copy-start = (bf16[512,640]{1,0:T(8,128)(2,1)S(1)}, bf16[512,640]{1,0:T(8,128)(2,1)}, u32[]{:S(2)}) copy-start(bf16[512,640]{1,0:T(8,128)(2,1)} %w_pred_ref.1) | copy-start | bytes 1966084

commit v2 on v1

--- a/solution.py
+++ b/solution.py
@@ -28,21 +28,49 @@
     return pl.BlockSpec(memory_space=pltpu.SMEM)
 
 
-def exchange_kernel(n_seq, enc_ref, pred_ref, w_enc_ref, w_pred_ref, frames_ref, a_ref, c_ref, send_sem, recv_sem):
+def exchange_kernel(n_seq, flen_ref, llen_ref, enc_ref, pred_ref, w_enc_ref, w_pred_ref, w_out_ref,
+                    order_ref, place_ref, frames_ref, own_pred_ref, a_ref, c_ref, w_out_t_ref,
+                    key_ref, sorted_ref, send_sem, recv_sem):
     seq = lax.axis_index("seq")
-    n_own = frames_ref.shape[1]
+    n_utt = enc_ref.shape[0]
+    n_own = n_utt // n_seq
     barrier = pltpu.get_barrier_semaphore()
     for hop in range(1, n_seq):
         pl.semaphore_signal(barrier, inc=1, device_id={"seq": lax.rem(seq + hop, n_seq)}, device_id_type=MESH)
-    frames_ref[pl.ds(seq, 1)] = enc_ref[pl.ds(seq * n_own, n_own)][None]
-    own_pred = pred_ref[pl.ds(seq * n_own, n_own)]
-    c_ref[...] = jnp.dot(own_pred.reshape(-1, own_pred.shape[-1]), w_pred_ref[...], preferred_element_type=F32).astype(BF16).astype(F32)
+
+    def set_key(i, carry):
+        key_ref[i] = ((flen_ref[i] + SUB - 1) // SUB) * ((llen_ref[i] + SUB) // SUB) * n_utt + i
+        return carry
+
+    def set_place(i, carry):
+        key = key_ref[i]
+        rank = jnp.int32(0)
+        for j in range(n_utt):
+            rank = rank + jnp.where(key_ref[j] > key, 1, 0)
+        deal = rank // n_seq
+        at = rank - deal * n_seq
+        at = jnp.where(deal % 2 == 0, at, n_seq - 1 - at)
+        place_ref[i] = at * n_own + deal
+        return carry
+
+    def set_order(k, carry):
+        utt = jnp.int32(0)
+        for j in range(n_utt):
+            utt = utt + jnp.where(place_ref[j] == k, j, 0)
+        order_ref[k] = utt
+        return carry
+
+    lax.fori_loop(0, n_utt, set_key, 0)
+    lax.fori_loop(0, n_utt, set_place, 0)
+    lax.fori_loop(0, n_utt, set_order, 0)
+    for k in range(n_utt):
+        sorted_ref[k] = enc_ref[order_ref[k]]
     pl.semaphore_wait(barrier, n_seq - 1)
     copies = []
     for hop in range(1, n_seq):
         peer = lax.rem(seq + hop, n_seq)
         copy = pltpu.make_async_remote_copy(
-            src_ref=enc_ref.at[pl.ds(peer * n_own, n_own)],
+            src_ref=sorted_ref.at[pl.ds(peer * n_own, n_own)],
             dst_ref=frames_ref.at[seq],
             send_sem=send_sem.at[hop - 1],
             recv_sem=recv_sem.at[hop - 1],
@@ -51,30 +79,45 @@
         )
         copy.start()
         copies.append(copy)
+    frames_ref[pl.ds(seq, 1)] = sorted_ref[pl.ds(seq * n_own, n_own)][None]
+    for j in range(n_own):
+        own_pred_ref[j] = pred_ref[order_ref[seq * n_own + j]]
+    own_pred = own_pred_ref[...]
+    c_ref[...] = jnp.dot(own_pred.reshape(-1, own_pred.shape[-1]), w_pred_ref[...], preferred_element_type=F32).astype(BF16).astype(F32)
+    w_out_t_ref[...] = w_out_ref[...].T
     for copy in copies:
         copy.wait()
     frames = frames_ref[...]
     a_ref[...] = jnp.dot(frames.reshape(-1, frames.shape[-1]), w_enc_ref[...], preferred_element_type=F32).astype(BF16).astype(F32)
 
 
-def exchange(n_seq, enc_loc, pred_loc, w_enc, w_pred):
+def exchange(n_seq, frame_len, label_len, enc_loc, pred_loc, w_enc, w_pred, w_out):
     n_utt, t_loc, width = enc_loc.shape
     n_own = n_utt // n_seq
     n_upos = pred_loc.shape[1]
-    joint = w_enc.shape[1]
+    joint, vocab = w_out.shape
     return pl.pallas_call(
         functools.partial(exchange_kernel, n_seq),
         out_shape=(
+            jax.ShapeDtypeStruct((n_utt,), jnp.int32),
+            jax.ShapeDtypeStruct((n_utt,), jnp.int32),
             jax.ShapeDtypeStruct((n_seq, n_own, t_loc, width), BF16),
+            jax.ShapeDtypeStruct((n_own, n_upos, width), BF16),
             jax.ShapeDtypeStruct((n_seq * n_own * t_loc, joint), F32),
             jax.ShapeDtypeStruct((n_own * n_upos, joint), F32),
+            jax.ShapeDtypeStruct((vocab, joint), BF16),
         ),
-        in_specs=[vspec()] * 4,
-        out_specs=(vspec(), vspec(), vspec()),
-        scratch_shapes=[pltpu.SemaphoreType.DMA((n_seq - 1,)), pltpu.SemaphoreType.DMA((n_seq - 1,))],
-        compiler_params=pltpu.CompilerParams(collective_id=0, has_side_effects=True, vmem_limit_bytes=VMEM_LIMIT),
+        in_specs=[sspec()] * 2 + [vspec()] * 5,
+        out_specs=(sspec(),) * 2 + (vspec(),) * 5,
+        scratch_shapes=[
+            pltpu.SMEM((n_utt,), jnp.int32),
+            VMEM(enc_loc.shape, BF16),
+            pltpu.SemaphoreType.DMA((n_seq - 1,)),
+            pltpu.SemaphoreType.DMA((n_seq - 1,)),
+        ],
+        compiler_params=pltpu.CompilerParams(collective_id=0, has_side_effects=True, vmem_limit_bytes=20_000_000),
         name="exchange",
-    )(enc_loc, pred_loc, w_enc, w_pred)
+    )(frame_len, label_len, enc_loc, pred_loc, w_enc, w_pred, w_out)
 
 
 def logaddexp(x, y):
@@ -82,7 +125,7 @@
     return top + jnp.log(1.0 + jnp.exp(-jnp.abs(x - y)))
 
 
-def lattice_kernel(n_own, n_frames, n_upos, seq_ref, flen_ref, llen_ref, labels_ref, a_ref, c_ref, w_ref, wt_ref,
+def lattice_kernel(n_own, n_frames, n_upos, seq_ref, order_ref, flen_ref, llen_ref, labels_ref, a_ref, c_ref, w_ref, wt_ref,
                    da_ref, dc_ref, gw_ref, loss_ref,
                    p_ref, h_ref, blank_ref, label_ref, alpha_ref, beta_ref, ids_ref, dact_ref, dpred_ref):
     vocab = w_ref.shape[1]
@@ -92,8 +135,9 @@
     rows_t = GROUPS * rows_g
     n_diag = n_frames + n_upos - 1
     first = seq_ref[0] * n_own
-    lens_t = [flen_ref[first + b] for b in range(n_own)]
-    lens_u = [llen_ref[first + b] for b in range(n_own)]
+    utts = [order_ref[first + b] for b in range(n_own)]
+    lens_t = [flen_ref[utt] for utt in utts]
+    lens_u = [llen_ref[utt] for utt in utts]
     blocks_t = [lax.div(n + SUB - 1, SUB) for n in lens_t]
     blocks_u = [lax.div(n + SUB, SUB) for n in lens_u]
     starts = [jnp.int32(0)]
@@ -117,7 +161,7 @@
     pos_col = lax.broadcasted_iota(jnp.int32, (n_upos, n_upos - 1), 0)
     pos_row = lax.broadcasted_iota(jnp.int32, (n_upos, n_upos - 1), 1)
     for b in range(n_own):
-        row = labels_ref[pl.ds(first + b, 1), :].astype(F32)
+        row = labels_ref[pl.ds(utts[b], 1), :].astype(F32)
         col = jnp.sum(jnp.where(pos_col == pos_row, row, 0.0), axis=1, keepdims=True)
         ids_ref[pl.ds(b * n_upos, n_upos), :] = jnp.broadcast_to(col, (n_upos, LANES)).astype(jnp.int32)
 
@@ -270,7 +314,7 @@
     dc_ref[...] = dpred_ref[...].astype(BF16)
 
 
-def lattice(n_seq, n_data, seq_idx, frame_len, label_len, labels, act, pred, w_out, w_out_t, n_upos, t_loc):
+def lattice(n_seq, n_data, seq_idx, order, frame_len, label_len, labels, act, pred, w_out, w_out_t, n_upos, t_loc):
     n_own = frame_len.shape[0] // n_seq
     n_frames = n_seq * t_loc
     joint, vocab = w_out.shape
@@ -285,7 +329,7 @@
             jax.ShapeDtypeStruct((n_data, joint, vocab // n_data), F32),
             jax.ShapeDtypeStruct((SUB, LANES), F32),
         ),
-        in_specs=[sspec(), sspec(), sspec()] + [vspec()] * 5,
+        in_specs=[sspec()] * 4 + [vspec()] * 5,
         out_specs=(vspec(),) * 4,
         scratch_shapes=[
             VMEM((cells, vocab), F32),
@@ -300,7 +344,7 @@
         ],
         compiler_params=pltpu.CompilerParams(vmem_limit_bytes=VMEM_LIMIT),
         name="lattice",
-    )(seq_idx, frame_len, label_len, labels, act, pred, w_out, w_out_t)
+    )(seq_idx, order, frame_len, label_len, labels, act, pred, w_out, w_out_t)
 
 
 class Copies:
@@ -381,15 +425,14 @@
         self.lb2.wait_recv()
 
 
-def combine_kernel(n_seq, n_data, frames_ref, pred_ref, da_ref, dc_ref, gw_ref, loss_ref,
-                   da_out, dc_out, gj_out, gw_out, loss_out,
-                   gj_acc, gw_acc, gj_pair, gw_pair, gj_py, gj_ly, gj_ry, gj_px, gj_lx, gj_rx, gw_px, gw_lx, gw_rx, gw_py, gw_ly, gw_ry, gj_mid, gw_mid,
+def combine_kernel(n_seq, n_data, frames_ref, pred_ref, w_enc_ref, da_ref, dc_ref, gw_ref, loss_ref,
+                   ge_out, dc_out, gj_out, gw_out, loss_out,
+                   gj_acc, gw_acc, gj_pair, gw_pair, gj_py, gj_ly, gj_ry, gj_px, gj_lx, gj_rx, gw_px, gw_lx, gw_rx, gw_py, gw_ly, gw_ry, gj_mid, gw_mid, ge_ref,
                    send_sem, recv_sem):
     seq = lax.axis_index("seq")
     y = lax.axis_index("data")
     x = lax.div(seq, CORES)
     core = lax.rem(seq, CORES)
-    n_own = frames_ref.shape[1]
     x_right = {"seq": lax.rem(x + 1, RING) * CORES + core}
     x_left = {"seq": lax.rem(x + RING - 1, RING) * CORES + core}
     y_right = {"data": lax.rem(y + 1, RING)}
@@ -403,10 +446,12 @@
 
     frames = frames_ref[...]
     contract_rows = (((0,), (0,)), ((), ()))
-    gj_acc[0] = lax.dot_general(frames.reshape(-1, frames.shape[-1]), da_ref[...].reshape(-1, da_ref.shape[-1]), contract_rows, preferred_element_type=F32)
-    own_pred = pred_ref[pl.ds(seq * n_own, n_own)]
+    gj_acc[0] = lax.dot_general(frames.reshape(-1, frames.shape[-1]), da_ref[...], contract_rows, preferred_element_type=F32)
+    own_pred = pred_ref[...]
     gj_acc[1] = lax.dot_general(own_pred.reshape(-1, own_pred.shape[-1]), dc_ref[...], contract_rows, preferred_element_type=F32)
-    da_out[pl.ds(seq, 1)] = da_ref[pl.ds(seq, 1)]
+    ge = lax.dot_general(da_ref[...], w_enc_ref[...], (((1,), (1,)), ((), ())), preferred_element_type=F32)
+    ge_ref[...] = ge.astype(BF16).reshape(ge_ref.shape)
+    ge_out[pl.ds(seq, 1)] = ge_ref[pl.ds(seq, 1)]
     dc_out[pl.ds(seq, 1)] = dc_ref[...][None]
     loss_out[pl.ds(seq, 1)] = loss_ref[...][None]
     pl.semaphore_wait(barrier, n_seq - 1 + 2)
@@ -431,7 +476,7 @@
     small = []
     for hop in range(1, n_seq):
         peer = lax.rem(seq + hop, n_seq)
-        small.append(copies.start(da_ref.at[peer], da_out.at[seq], {"seq": peer}))
+        small.append(copies.start(ge_ref.at[peer], ge_out.at[seq], {"seq": peer}))
         small.append(copies.start(loss_ref, loss_out.at[seq], {"seq": peer}))
 
     gj_row = pl.multiple_of(core * gj_half, gj_half)
@@ -546,8 +591,8 @@
 N_COPIES = 6 + 2 + 4 + 14 + 4 * 6 + 4 * 6 + 8
 
 
-def combine(n_seq, n_data, frames, pred_loc, da, dc, gw, loss):
-    _, n_own, t_loc, width = frames.shape
+def combine(n_seq, n_data, frames, own_pred, w_enc, da, dc, gw, loss):
+    width = frames.shape[-1]
     joint = da.shape[-1]
     n_cols, _, col = gw.shape
     gj_half, gw_half = width // CORES, joint // CORES
@@ -556,13 +601,13 @@
     return pl.pallas_call(
         functools.partial(combine_kernel, n_seq, n_data),
         out_shape=(
-            jax.ShapeDtypeStruct((n_seq, n_own, t_loc, joint), BF16),
+            jax.ShapeDtypeStruct(frames.shape, BF16),
             jax.ShapeDtypeStruct((n_seq,) + dc.shape, BF16),
             jax.ShapeDtypeStruct((2, width, joint), F32),
             jax.ShapeDtypeStruct(gw.shape, F32),
             jax.ShapeDtypeStruct((n_seq,) + loss.shape, F32),
         ),
-        in_specs=[vspec()] * 6,
+        in_specs=[vspec()] * 7,
         out_specs=(vspec(),) * 5,
         scratch_shapes=[
             VMEM((2, width, joint), F32),
@@ -577,12 +622,70 @@
         + [
             VMEM((2, gj_y, joint), F32),
             VMEM((n_cols, gw_x, col), F32),
+            VMEM(frames.shape, BF16),
             pltpu.SemaphoreType.DMA((N_COPIES,)),
             pltpu.SemaphoreType.DMA((N_COPIES,)),
         ],
-        compiler_params=pltpu.CompilerParams(collective_id=1, has_side_effects=True, vmem_limit_bytes=VMEM_LIMIT),
+        compiler_params=pltpu.CompilerParams(collective_id=1, has_side_effects=True, vmem_limit_bytes=40_000_000),
         name="combine",
-    )(frames, pred_loc, da.reshape(n_seq, n_own, t_loc, joint), dc, gw, loss)
+    )(frames, own_pred, w_enc, da, dc, gw, loss)
+
+
+def output_kernel(place_ref, losses_ref, ge_ref, dc_ref, w_pred_ref, gj_ref, gw_ref,
+                  loss_out, ge_out, gp_out, gwe_out, gwp_out, gwo_out, rows_ref, gp_ref, sem):
+    n_utt, n_upos, width = gp_out.shape
+    n_own = ge_ref.shape[1]
+    n_cols, _, col = gw_ref.shape
+    copies = [pltpu.make_async_copy(gj_ref.at[0], gwe_out, sem.at[0]), pltpu.make_async_copy(gj_ref.at[1], gwp_out, sem.at[1])]
+    for k in range(n_cols):
+        copies.append(pltpu.make_async_copy(gw_ref.at[k], gwo_out.at[:, pl.ds(k * col, col)], sem.at[2 + k]))
+    for copy in copies:
+        copy.start()
+    n_parts = 4
+    part = n_utt // n_parts
+    for p in range(n_parts):
+        for i in range(p * part, (p + 1) * part):
+            place = place_ref[i]
+            dev = place // n_own
+            own = place - dev * n_own
+            loss_out[i] = losses_ref[dev, 0, own]
+            ge_out[i] = ge_ref[dev, own]
+            rows_ref[i] = dc_ref[dev, pl.ds(pl.multiple_of(own * n_upos, n_upos), n_upos), :]
+        rows = rows_ref[p * part:(p + 1) * part]
+        grads = lax.dot_general(rows.reshape(part * n_upos, -1), w_pred_ref[...], (((1,), (1,)), ((), ())), preferred_element_type=F32)
+        gp_ref[p * part:(p + 1) * part] = grads.reshape(part, n_upos, width)
+        copy = pltpu.make_async_copy(gp_ref.at[pl.ds(p * part, part)], gp_out.at[pl.ds(p * part, part)], sem.at[2 + n_cols + p])
+        copy.start()
+        copies.append(copy)
+    for copy in copies:
+        copy.wait()
+
+
+def outputs(place, losses, ge, dc, w_pred, gj, gw, n_upos):
+    n_seq, n_own, t_loc, width = ge.shape
+    n_utt = n_seq * n_own
+    n_cols, joint, col = gw.shape
+    hbm = pl.BlockSpec(memory_space=pl.ANY)
+    return pl.pallas_call(
+        output_kernel,
+        out_shape=(
+            jax.ShapeDtypeStruct((n_utt,), F32),
+            jax.ShapeDtypeStruct((n_utt, t_loc, width), BF16),
+            jax.ShapeDtypeStruct((n_utt, n_upos, width), F32),
+            jax.ShapeDtypeStruct((width, joint), F32),
+            jax.ShapeDtypeStruct((width, joint), F32),
+            jax.ShapeDtypeStruct((joint, n_cols * col), F32),
+        ),
+        in_specs=[sspec()] * 2 + [vspec()] * 5,
+        out_specs=(sspec(), vspec()) + (hbm,) * 4,
+        scratch_shapes=[
+            VMEM((n_utt, n_upos, joint), BF16),
+            VMEM((n_utt, n_upos, width), F32),
+            pltpu.SemaphoreType.DMA((2 + n_cols + 4,)),
+        ],
+        compiler_params=pltpu.CompilerParams(vmem_limit_bytes=20_000_000),
+        name="outputs",
+    )(place, losses, ge, dc, w_pred, gj, gw)
 
 
 def solution(mesh):
@@ -596,17 +699,13 @@
     weight_out = P("part", None)
 
     def body(enc_loc, pred_loc, w_enc, w_pred, w_out, labels, frame_len, label_len):
-        n_utt, t_loc, width = enc_loc.shape
-        n_own = n_utt // n_seq
+        t_loc = enc_loc.shape[1]
         n_upos = pred_loc.shape[1]
-        joint, vocab = w_out.shape
         seq_idx = lax.axis_index("seq").astype(jnp.int32).reshape(1)
-        frames, act, pred = exchange(n_seq, enc_loc, pred_loc, w_enc, w_pred)
-        da, dc, gw, loss = lattice(n_seq, n_data, seq_idx, frame_len, label_len, labels, act, pred, w_out, w_out.T, n_upos, t_loc)
-        da_loc, dc_all, gj, gw, loss_all = combine(n_seq, n_data, frames, pred_loc, da, dc, gw, loss)
-        grad_enc = jnp.einsum("btj,hj->bth", da_loc.reshape(n_utt, t_loc, joint), w_enc, preferred_element_type=F32).astype(BF16)
-        grad_pred = jnp.einsum("buj,hj->buh", dc_all.reshape(n_utt, n_upos, joint), w_pred, preferred_element_type=F32)
-        grad_w_out = jnp.swapaxes(gw, 0, 1).reshape(joint, vocab)
-        return loss_all[:, 0, :n_own].reshape(n_utt), grad_enc, grad_pred, gj[0], gj[1], grad_w_out
+        order, place, frames, own_pred, act, pred, w_out_t = exchange(n_seq, frame_len, label_len, enc_loc, pred_loc, w_enc, w_pred, w_out)
+        da, dc, gw, loss = lattice(n_seq, n_data, seq_idx, order, frame_len, label_len, labels, act, pred, w_out, w_out_t, n_upos, t_loc)
+        ge, dc_all, gj, gw, losses = combine(n_seq, n_data, frames, own_pred, w_enc, da, dc, gw, loss)
+        loss, grad_enc, grad_pred, gw_enc, gw_pred, gw_out = outputs(place, losses, ge, dc_all, w_pred, gj, gw, n_upos)
+        return loss, grad_enc, grad_pred, gw_enc, gw_pred, gw_out
 
     return jax.shard_map(body, mesh=mesh, in_specs=(enc_spec, utt_cube, weight_in, weight_in, weight_in, utt_mats, utt_rows, utt_rows), out_specs=(utt_rows, enc_spec, utt_cube, weight_out, weight_out, weight_out), check_vma=False)

time: 145 us -> 139 us (0.959)
  Pallas kernels: 127 us -> 119 us
  local copies, waits for them, and re-layouts: 11.5 us -> 18.8 us
  matrix products: 5.94 us -> 0 us
    pallas_call x1, Pallas kernels: 77.4 us -> 55.2 us  [combine(): pl.pallas_call(functools.partial(combine_kernel, n_seq, n_data), out_shap...]
    unnamed x4 -> x42, local copies, waits for them, and re-layouts: 4.52 us -> 18.8 us
    pallas_call x1, Pallas kernels: 37.1 us -> 45 us  [lattice(): pl.pallas_call(functools.partial(lattice_kernel, n_own, n_frames, n_upos)...]
    dot_general x2 -> x0, matrix products: 5.94 us -> none  [the longest x1 3.64 us: body(): jnp.einsum('buj,hj->buh', dc_all.reshape(n_utt, n_upos, joint), w_pred, p...]
    pallas_call x0 -> x1, Pallas kernels: none -> 5.32 us  [outputs(): pl.pallas_call(output_kernel, out_shape=(jax.ShapeDtypeStruct((n_utt,), F...]
    squeeze x1 -> x0, local copies, waits for them, and re-layouts: 3.37 us -> none  [body(): gj[1]]
    transpose x1 -> x0, local copies, waits for them, and re-layouts: 2.15 us -> none  [body(): grad_w_out = jnp.swapaxes(gw, 0, 1).reshape(joint, vocab)]
where the time goes in v2:
time: 139 us; the launch traced here: 138 us
  Pallas kernels  119 us (86%)
  local copies, waits for them, and re-layouts  18.8 us (14%)
    pallas_call x1, Pallas kernels, combine(): pl.pallas_call(functools.partial(combine_kernel, n_seq, n_data), out_shap...  55.2 us
    pallas_call x1, Pallas kernels, lattice(): pl.pallas_call(functools.partial(lattice_kernel, n_own, n_frames, n_upos)...  45 us
    unnamed x42, local copies, waits for them, and re-layouts  18.8 us
    pallas_call x1, Pallas kernels, exchange(): pl.pallas_call(functools.partial(exchange_kernel, n_seq), out_shape=(jax....  13 us
    pallas_call x1, Pallas kernels, outputs(): pl.pallas_call(output_kernel, out_shape=(jax.ShapeDtypeStruct((n_utt,), F...  5.32 us

profile of v2, /device:TPU:97, one launch (start us, length us, event | category | flops | bytes accessed | tf_op | source)
XLA Modules:
  0.0 138.0 jit_solution(2499245892165665795)
XLA Ops:
  0.6 0.0 copy-start
  0.6 1.3 copy-done
  2.0 0.0 copy-start.2
  2.0 1.1 copy-done.2
  3.0 0.0 copy-start.4
  3.0 1.1 copy-done.4
  4.1 0.0 copy-start.7
  4.1 1.2 copy-done.7
  5.4 0.0 copy-start.11
  5.4 0.9 copy-done.11
  6.3 0.0 copy-start.18
  6.3 0.7 copy-done.18
  7.0 0.7 copy-done.19
  7.6 13.0 %exchange.1 = (s32[32]{0:T(128)S(1)}, s32[32]{0:T(128)S(1)}, bf16[8,4,8,512]{3,2,1,0:T(8,128)(2,1)S(1)}, bf16[4,32,512]{2,1,0:T(8,128)(2,1)S(1)}, f32[256,640]{1...) custom-call(s32[32]{0:T(128)S(1)} %copy-done.18, s32[32]{0:T(128)S(1)} %copy-done.19, ...), custom_call_target="tpu_custom_call" | custom-call | tf_op jit(solution)/shard_map/exchange/pallas_call | solution.py:99
  20.7 0.0 copy-start.6
  20.7 1.0 copy-done.6
  21.7 0.8 copy-done.8
  22.6 0.7 copy-done.10
  23.3 0.7 copy-done.12
  24.0 0.7 copy-done.15
  24.6 0.6 copy-done.20
  25.2 45.0 %lattice.1 = (bf16[256,640]{1,0:T(8,128)(2,1)}, bf16[128,640]{1,0:T(8,128)(2,1)}, f32[4,640,256]{2,1,0:T(8,128)}, f32[8,128]{1,0:T(8,128)}) custom-call(s32[1]{0:T(128)} %bitcast.seq_ref, s32[32]{0:T(128)} %copy-done.20, s32[32]{0:T(128)} %flen_ref.3, s32[32]{0:T(128)} %llen_ref.3, s32[32,31]{1,0:T(8,128)} %labels_ref.1, f32[256,640]{1,0:T(8,128)} %copy-done.8, ...), custom_call_target="tpu_custom_call" | custom-call | tf_op jit(solution)/shard_map/lattice/pallas_call | solution.py:324
  70.3 1.7 %copy-done.1 = f32[4,640,256]{2,1,0:T(8,128)S(1)} copy-done((f32[4,640,256]{2,1,0:T(8,128)S(1)}, f32[4,640,256]{2,1,0:T(8,128)}, u32[]{:S(2)}) %copy-start.1) | copy-done | bytes 2621464
  72.0 1.1 copy-done.3
  73.1 1.0 copy-done.9
  74.1 0.9 copy-done.13
  75.0 0.9 copy-done.14
  75.9 0.9 copy-done.16
  76.8 0.7 copy-done.17
  77.5 55.2 %combine.1 = (bf16[8,4,8,512]{3,2,1,0:T(8,128)(2,1)S(1)}, bf16[8,128,640]{2,1,0:T(8,128)(2,1)S(1)}, f32[2,512,640]{2,1,0:T(8,128)S(1)}, f32[4,640,256]{2,1,0:T(8,128)S(1)}, f32[8,8,128]{2,1,0:T(8,128)S(1)}) custom-call(bf16[8,4,8,512]{3,2,1,0:T(8,128)(2,1)S(1)} %copy-done.13, bf16[4,32,512]{2,1,0:T(8,128)(2,1)S(1)} %copy-done.16, ...), custom_call_target="tpu_custom_call" | custom-call | tf_op jit(solution)/shard_map/combine/pallas_call | solution.py:601
  132.7 0.0 copy-done.5
  132.7 5.3 %outputs.1 = (f32[32]{0:T(128)}, bf16[32,8,512]{2,1,0:T(8,128)(2,1)}, f32[32,32,512]{2,1,0:T(8,128)}, f32[512,640]{1,0:T(8,128)}, f32[512,640]{1,0:T(8,128)}, /*index=5*/f32[640,1024]{1,0:T(8,128)}) custom-call(s32[32]{0:T(128)S(1)} %get-tuple-element.22.place_ref, f32[8,8,128]{2,1,0:T(8,128)S(1)} %get-tuple-element.33.losses_ref, ...), custom_call_target="tpu_custom_call" | custom-call | tf_op jit(solution)/shard_map/outputs/pallas_call | solution.py:669
  (14 shorter events, 0.0 us)
Async XLA Ops:
  0.6 1.3 copy-start
  2.0 1.1 copy-start.2
  3.0 1.1 copy-start.4
  4.1 1.2 copy-start.7
  5.4 0.9 copy-start.11
  6.3 0.7 copy-start.18
  7.0 0.7 copy-start.19
  20.7 1.1 copy-start.6
  21.7 0.8 copy-start.8
  22.5 0.7 copy-start.10
  23.3 0.7 copy-start.12
  24.0 0.7 copy-start.15
  24.6 0.6 copy-start.20
  70.3 1.7 %copy-start.1 = (f32[4,640,256]{2,1,0:T(8,128)S(1)}, f32[4,640,256]{2,1,0:T(8,128)}, u32[]{:S(2)}) copy-start(f32[4,640,256]{2,1,0:T(8,128)} %get-tuple-element.31.gw_ref) | copy-start | bytes 7864324
  72.0 1.1 copy-start.3
  73.1 1.0 copy-start.9
  74.1 0.9 copy-start.13
  75.0 0.9 copy-start.14
  75.9 0.9 copy-start.16
  76.8 0.7 copy-start.17
  77.5 55.2 %copy-start.5 = (bf16[512,640]{1,0:T(8,128)(2,1)S(1)}, bf16[512,640]{1,0:T(8,128)(2,1)}, u32[]{:S(2)}) copy-start(bf16[512,640]{1,0:T(8,128)(2,1)} %w_pred_ref.3) | copy-start | bytes 1966084

commit v3 on v2

--- a/solution.py
+++ b/solution.py
@@ -15,7 +15,8 @@
 VMEM_LIMIT = 67_000_000
 SUB = 8
 LANES = 128
-GROUPS = 8
+GROUPS = 4
+BLOCK = 32
 CORES = 2
 RING = 4
 
@@ -115,7 +116,7 @@
             pltpu.SemaphoreType.DMA((n_seq - 1,)),
             pltpu.SemaphoreType.DMA((n_seq - 1,)),
         ],
-        compiler_params=pltpu.CompilerParams(collective_id=0, has_side_effects=True, vmem_limit_bytes=20_000_000),
+        compiler_params=pltpu.CompilerParams(collective_id=0, has_side_effects=True, vmem_limit_bytes=VMEM_LIMIT),
         name="exchange",
     )(frame_len, label_len, enc_loc, pred_loc, w_enc, w_pred, w_out)
 
@@ -127,7 +128,7 @@
 
 def lattice_kernel(n_own, n_frames, n_upos, seq_ref, order_ref, flen_ref, llen_ref, labels_ref, a_ref, c_ref, w_ref, wt_ref,
                    da_ref, dc_ref, gw_ref, loss_ref,
-                   p_ref, h_ref, blank_ref, label_ref, alpha_ref, beta_ref, ids_ref, dact_ref, dpred_ref):
+                   e_ref, h_ref, blank_ref, label_ref, alpha_ref, beta_ref, ids_ref, dact_ref, dpred_ref, work0, work1, dz0, dz1):
     vocab = w_ref.shape[1]
     joint = w_ref.shape[0]
     n_vt = vocab // LANES
@@ -172,49 +173,78 @@
     dpred_ref[...] = jnp.zeros_like(dpred_ref)
 
     lane = lax.broadcasted_iota(jnp.int32, (SUB, LANES), 1)
-    vocab_lane = lax.broadcasted_iota(jnp.int32, (rows_t, LANES), 1)
-
-    def tile_ids(groups):
-        parts = []
-        for _, b, ti, ui in groups:
-            ids = ids_ref[pl.ds(pl.multiple_of(b * n_upos + ui * SUB, SUB), SUB), :]
-            parts.append(jnp.broadcast_to(ids[None], (SUB, SUB, LANES)).reshape(rows_g, LANES))
-        return jnp.concatenate(parts, axis=0)
-
-    def cell_row(ti, k, ui):
-        return pl.multiple_of((n_diag - 1 - ti * SUB - k) * n_upos + ui * SUB, SUB)
-
-    def forward(i, carry):
-        groups = [decode(i * GROUPS + g) for g in range(GROUPS)]
-        parts = []
-        for g, (n, b, ti, ui) in enumerate(groups):
-            a8 = a_ref[pl.ds(pl.multiple_of((ti * n_own + b) * SUB, SUB), SUB), :]
-            c8 = c_ref[pl.ds(pl.multiple_of(b * n_upos + ui * SUB, SUB), SUB), :]
-            parts.append(jnp.tanh(a8[:, None, :] + c8[None, :, :]).reshape(rows_g, joint).astype(BF16))
-        h = jnp.concatenate(parts, axis=0)
-        row0 = pl.multiple_of(i * rows_t, rows_t)
-        h_ref[pl.ds(row0, rows_t), :] = h
-        z = jnp.dot(h, w_ref[...], preferred_element_type=F32)
-        top = jnp.max(z, axis=1, keepdims=True)
-        e = jnp.exp(z - top)
-        norm = jnp.sum(e, axis=1, keepdims=True)
-        p_ref[pl.ds(row0, rows_t), :] = e * (1.0 / norm)
-        log_norm = top + jnp.log(norm)
-        ids = tile_ids(groups)
-        picked = jnp.zeros((rows_t, LANES), F32)
-        for v in range(n_vt):
-            picked = picked + jnp.where(vocab_lane + v * LANES == ids, z[:, v * LANES:(v + 1) * LANES], 0.0)
-        label = jnp.sum(picked, axis=1, keepdims=True) - log_norm
-        blank = z[:, 0:1] - log_norm
-        for g, (n, b, ti, ui) in enumerate(groups):
-            for k in range(SUB):
-                at = cell_row(ti, k, ui)
-                lo = g * rows_g + k * SUB
-                blank_ref[pl.ds(at, SUB), :] = jnp.where(lane == b, blank[lo:lo + SUB], blank_ref[pl.ds(at, SUB), :])
-                label_ref[pl.ds(at, SUB), :] = jnp.where(lane == b, label[lo:lo + SUB], label_ref[pl.ds(at, SUB), :])
+    block_lane = lax.broadcasted_iota(jnp.int32, (BLOCK, LANES), 1)
+    t_block = BLOCK // SUB
+    works, dzs = (work0, work1), (dz0, dz1)
+
+    def tile_rows(i):
+        return pl.ds(pl.multiple_of(jnp.clip(i, 0, n_tiles - 1) * rows_t, rows_t), rows_t)
+
+    def tile_groups(i):
+        return [decode(jnp.clip(i, 0, n_tiles - 1) * GROUPS + g) for g in range(GROUPS)]
+
+    def pred_row(b, ui):
+        return pl.ds(pl.multiple_of(b * n_upos + ui * SUB, SUB), SUB)
+
+    def act_row(b, ti):
+        return pl.ds(pl.multiple_of((ti * n_own + b) * SUB, SUB), SUB)
+
+    def block_ids(b, ui):
+        ids = ids_ref[pred_row(b, ui), :]
+        return jnp.broadcast_to(ids[None], (t_block, SUB, LANES)).reshape(BLOCK, LANES)
+
+    def cell_rows(ti, k, ui):
+        return pl.ds(pl.multiple_of((n_diag - 1 - ti * SUB - k) * n_upos + ui * SUB, SUB), SUB)
+
+    def make_hidden(i):
+        first_row = jnp.clip(i, 0, n_tiles - 1) * rows_t
+        for g, (n, b, ti, ui) in enumerate(tile_groups(i)):
+            a8 = a_ref[act_row(b, ti), :]
+            c8 = c_ref[pred_row(b, ui), :]
+            h = jnp.tanh(a8[:, None, :] + c8[None, :, :]).reshape(rows_g, joint).astype(BF16)
+            h_ref[pl.ds(pl.multiple_of(first_row + g * rows_g, rows_g), rows_g), :] = h
+
+    def make_logits(i, z_ref):
+        z_ref[...] = jnp.dot(h_ref[tile_rows(i), :], w_ref[...], preferred_element_type=F32)
+
+    def make_softmax(i, z_ref):
+        first_row = jnp.clip(i, 0, n_tiles - 1) * rows_t
+        for g, (n, b, ti, ui) in enumerate(tile_groups(i)):
+            ids = block_ids(b, ui)
+            for r in range(0, rows_g, BLOCK):
+                z = z_ref[g * rows_g + r:g * rows_g + r + BLOCK, :]
+                top = jnp.max(z, axis=1, keepdims=True)
+                e = jnp.exp(z - top)
+                norm = jnp.sum(e, axis=1, keepdims=True)
+                e_ref[pl.ds(pl.multiple_of(first_row + g * rows_g + r, BLOCK), BLOCK), :] = e
+                log_norm = top + jnp.log(norm)
+                picked = jnp.zeros((BLOCK, LANES), F32)
+                for v in range(n_vt):
+                    picked = picked + jnp.where(block_lane + v * LANES == ids, z[:, v * LANES:(v + 1) * LANES], 0.0)
+                label = jnp.sum(picked, axis=1, keepdims=True) - log_norm
+                blank = z[:, 0:1] - log_norm
+                scale = 1.0 / norm
+                rows = [cell_rows(ti, r // SUB + k, ui) for k in range(t_block)]
+                old_blank = [blank_ref[at, :] for at in rows]
+                old_label = [label_ref[at, :] for at in rows]
+                for k, at in enumerate(rows):
+                    sl = slice(k * SUB, (k + 1) * SUB)
+                    blank_ref[at, :] = jnp.where(lane == b, blank[sl], jnp.where(lane == b + n_own, scale[sl], old_blank[k]))
+                    label_ref[at, :] = jnp.where(lane == b, label[sl], old_label[k])
+
+    make_hidden(0)
+    make_logits(0, work0)
+    make_hidden(1)
+
+    def forward(j, carry):
+        for half in range(2):
+            i = 2 * j + half
+            make_logits(i + 1, works[1 - half])
+            make_softmax(i, works[half])
+            make_hidden(i + 2)
         return carry
 
-    lax.fori_loop(0, n_tiles, forward, 0)
+    lax.fori_loop(0, lax.div(n_tiles + 1, 2), forward, 0)
 
     upos = lax.broadcasted_iota(jnp.int32, (n_upos, LANES), 0)
     utt = lax.broadcasted_iota(jnp.int32, (n_upos, LANES), 1)
@@ -263,53 +293,72 @@
         alpha = alpha_ref[d]
         after = beta_ref[d + 1]
         cell_ok = (t >= 0) & (t < t_end) & (upos <= u_end)
-        q0 = jnp.where(cell_ok, jnp.exp(alpha + blank_ref[diagonal(d), :] + after - log_prob), 0.0)
+        blank = blank_ref[diagonal(d), :]
+        q0 = jnp.where(cell_ok, jnp.exp(alpha + blank + after - log_prob), 0.0)
         q1 = jnp.where(cell_ok & (upos < u_end), jnp.exp(alpha + label_ref[diagonal(d), :] + up(after) - log_prob), 0.0)
-        blank_ref[diagonal(d), :] = q0
+        blank_ref[diagonal(d), :] = jnp.where(utt < n_own, q0, blank)
         label_ref[diagonal(d), :] = q1
         return carry
 
     lax.fori_loop(0, n_diag, occupancy, 0)
 
-    def backward(i, carry):
-        groups = [decode(i * GROUPS + g) for g in range(GROUPS)]
-        row0 = pl.multiple_of(i * rows_t, rows_t)
-        q0s, q1s = [], []
-        for g, (n, b, ti, ui) in enumerate(groups):
+    def make_dz(i, dz_ref):
+        first_row = jnp.clip(i, 0, n_tiles - 1) * rows_t
+        for g, (n, b, ti, ui) in enumerate(tile_groups(i)):
             keep = (lane == b) & (i * GROUPS + g < total)
-            for k in range(SUB):
-                at = cell_row(ti, k, ui)
-                q0s.append(jnp.where(keep, blank_ref[pl.ds(at, SUB), :], 0.0))
-                q1s.append(jnp.where(keep, label_ref[pl.ds(at, SUB), :], 0.0))
-        q0 = jnp.sum(jnp.concatenate(q0s, axis=0), axis=1, keepdims=True)
-        q1 = jnp.sum(jnp.concatenate(q1s, axis=0), axis=1, keepdims=True)
-        both = q0 + q1
-        ids = tile_ids(groups)
-        cols = []
-        for v in range(n_vt):
-            at_v = vocab_lane + v * LANES
-            dz = p_ref[pl.ds(row0, rows_t), v * LANES:(v + 1) * LANES] * both
-            if v == 0:
-                dz = dz - jnp.where(at_v == 0, q0, 0.0)
-            dz = dz - jnp.where(at_v == ids, q1, 0.0)
-            cols.append(dz.astype(BF16))
-        dz = jnp.concatenate(cols, axis=1)
-        h = h_ref[pl.ds(row0, rows_t), :]
-        dh = jnp.dot(dz, wt_ref[...], preferred_element_type=F32)
-        hf = h.astype(F32)
-        ds = dh * (1.0 - hf * hf)
-        for g, (n, b, ti, ui) in enumerate(groups):
-            cube = ds[g * rows_g:(g + 1) * rows_g].reshape(SUB, SUB, joint)
-            at = pl.multiple_of((ti * n_own + b) * SUB, SUB)
-            dact_ref[pl.ds(at, SUB), :] += jnp.sum(cube, axis=1)
-            at = pl.multiple_of(b * n_upos + ui * SUB, SUB)
-            dpred_ref[pl.ds(at, SUB), :] += jnp.sum(cube, axis=0)
+            ids = block_ids(b, ui)
+            for r in range(0, rows_g, BLOCK):
+                q0s, q1s, scales = [], [], []
+                for k in range(t_block):
+                    at = cell_rows(ti, r // SUB + k, ui)
+                    blank = blank_ref[at, :]
+                    q0s.append(jnp.where(keep, blank, 0.0))
+                    scales.append(jnp.where(lane == b + n_own, blank, 0.0))
+                    q1s.append(jnp.where(keep, label_ref[at, :], 0.0))
+                q0 = jnp.sum(jnp.concatenate(q0s, axis=0), axis=1, keepdims=True)
+                q1 = jnp.sum(jnp.concatenate(q1s, axis=0), axis=1, keepdims=True)
+                scale = jnp.sum(jnp.concatenate(scales, axis=0), axis=1, keepdims=True) * (q0 + q1)
+                rows = pl.ds(pl.multiple_of(first_row + g * rows_g + r, BLOCK), BLOCK)
+                for v in range(n_vt):
+                    at_v = block_lane + v * LANES
+                    dz = e_ref[rows, v * LANES:(v + 1) * LANES] * scale
+                    if v == 0:
+                        dz = dz - jnp.where(at_v == 0, q0, 0.0)
+                    dz = dz - jnp.where(at_v == ids, q1, 0.0)
+                    dz_ref[g * rows_g + r:g * rows_g + r + BLOCK, v * LANES:(v + 1) * LANES] = dz.astype(BF16)
+
+    def make_products(i, dz_ref, dh_ref):
+        dz = dz_ref[...]
+        dh_ref[:, :joint] = jnp.dot(dz, wt_ref[...], preferred_element_type=F32)
+        h = h_ref[tile_rows(i), :]
         for y in range(gw_ref.shape[0]):
             part = dz[:, y * gw_ref.shape[2]:(y + 1) * gw_ref.shape[2]]
             gw_ref[y] += lax.dot_general(h, part, (((0,), (0,)), ((), ())), preferred_element_type=F32)
+
+    def make_sums(i, dh_ref):
+        first_row = jnp.clip(i, 0, n_tiles - 1) * rows_t
+        for g, (n, b, ti, ui) in enumerate(tile_groups(i)):
+            rows = pl.ds(pl.multiple_of(first_row + g * rows_g, rows_g), rows_g)
+            for v in range(joint // LANES):
+                cols = slice(v * LANES, (v + 1) * LANES)
+                h = h_ref[rows, cols].astype(F32)
+                ds = dh_ref[g * rows_g:(g + 1) * rows_g, cols] * (1.0 - h * h)
+                cube = ds.reshape(SUB, SUB, LANES)
+                dact_ref[act_row(b, ti), cols] += jnp.sum(cube, axis=1)
+                dpred_ref[pred_row(b, ui), cols] += jnp.sum(cube, axis=0)
+
+    work1[...] = jnp.zeros_like(work1)
+    make_dz(0, dz0)
+
+    def backward(j, carry):
+        for half in range(2):
+            i = 2 * j + half
+            make_products(i, dzs[half], works[half])
+            make_dz(i + 1, dzs[1 - half])
+            make_sums(i - 1, works[1 - half])
         return carry
 
-    lax.fori_loop(0, n_tiles, backward, 0)
+    lax.fori_loop(0, lax.div(n_tiles + 2, 2), backward, 0)
     da_ref[...] = dact_ref[...].astype(BF16)
     dc_ref[...] = dpred_ref[...].astype(BF16)
 
@@ -341,6 +390,10 @@
             VMEM((n_own * n_upos, LANES), jnp.int32),
             VMEM(act.shape, F32),
             VMEM(pred.shape, F32),
+            VMEM((GROUPS * SUB * SUB, vocab), F32),
+            VMEM((GROUPS * SUB * SUB, vocab), F32),
+            VMEM((GROUPS * SUB * SUB, vocab), BF16),
+            VMEM((GROUPS * SUB * SUB, vocab), BF16),
         ],
         compiler_params=pltpu.CompilerParams(vmem_limit_bytes=VMEM_LIMIT),
         name="lattice",
@@ -626,7 +679,7 @@
             pltpu.SemaphoreType.DMA((N_COPIES,)),
             pltpu.SemaphoreType.DMA((N_COPIES,)),
         ],
-        compiler_params=pltpu.CompilerParams(collective_id=1, has_side_effects=True, vmem_limit_bytes=40_000_000),
+        compiler_params=pltpu.CompilerParams(collective_id=1, has_side_effects=True, vmem_limit_bytes=VMEM_LIMIT),
         name="combine",
     )(frames, own_pred, w_enc, da, dc, gw, loss)
 
@@ -683,7 +736,7 @@
             VMEM((n_utt, n_upos, width), F32),
             pltpu.SemaphoreType.DMA((2 + n_cols + 4,)),
         ],
-        compiler_params=pltpu.CompilerParams(vmem_limit_bytes=20_000_000),
+        compiler_params=pltpu.CompilerParams(vmem_limit_bytes=VMEM_LIMIT),
         name="outputs",
     )(place, losses, ge, dc, w_pred, gj, gw)
 

time: 139 us -> 127 us (0.914); the launches traced: 138 us -> 128 us
  local copies, waits for them, and re-layouts: 18.8 us -> 0 us
  Pallas kernels: 119 us -> 127 us
    unnamed x42 -> x0, local copies, waits for them, and re-layouts: 18.8 us -> none
    pallas_call x1, Pallas kernels: 55.2 us -> 59.9 us  [combine(): pl.pallas_call(functools.partial(combine_kernel, n_seq, n_data), out_shap...]
    pallas_call x1, Pallas kernels: 13 us -> 15.6 us  [exchange(): pl.pallas_call(functools.partial(exchange_kernel, n_seq), out_shape=(jax....]
    pallas_call x1, Pallas kernels: 5.32 us -> 7.03 us  [outputs(): pl.pallas_call(output_kernel, out_shape=(jax.ShapeDtypeStruct((n_utt,), F...]
where the time goes in v3:
time: 127 us; the launch traced here: 128 us
  Pallas kernels  127 us (100%)
    pallas_call x1, Pallas kernels, combine(): pl.pallas_call(functools.partial(combine_kernel, n_seq, n_data), out_shap...  59.9 us
    pallas_call x1, Pallas kernels, lattice(): pl.pallas_call(functools.partial(lattice_kernel, n_own, n_frames, n_upos)...  44.6 us
    pallas_call x1, Pallas kernels, exchange(): pl.pallas_call(functools.partial(exchange_kernel, n_seq), out_shape=(jax....  15.6 us
    pallas_call x1, Pallas kernels, outputs(): pl.pallas_call(output_kernel, out_shape=(jax.ShapeDtypeStruct((n_utt,), F...  7.03 us

profile of v3, /device:TPU:97, one launch (start us, length us, event | category | flops | bytes accessed | tf_op | source)
XLA Modules:
  0.0 127.7 jit_solution(17506440804977074239)
XLA Ops:
  0.6 15.6 %exchange.1 = (s32[32]{0:T(128)}, s32[32]{0:T(128)}, bf16[8,4,8,512]{3,2,1,0:T(8,128)(2,1)}, bf16[4,32,512]{2,1,0:T(8,128)(2,1)}, f32[256,640]{1,0:T(8,128)}, /*...) custom-call(s32[32]{0:T(128)} %flen_ref.3, s32[32]{0:T(128)} %llen_ref.3, bf16[32,8,512]{2,1,0:T(8,128)(2,1)} %enc_ref.1, ...), custom_call_target="tpu_custom_call" | custom-call | tf_op jit(solution)/shard_map/exchange/pallas_call | solution.py:100
  16.2 44.6 %lattice.1 = (bf16[256,640]{1,0:T(8,128)(2,1)}, bf16[128,640]{1,0:T(8,128)(2,1)}, f32[4,640,256]{2,1,0:T(8,128)}, f32[8,128]{1,0:T(8,128)}) custom-call(s32[1]{0:T(128)} %bitcast.seq_ref, s32[32]{0:T(128)} %get-tuple-element.25.order_ref, s32[32]{0:T(128)} %flen_ref.3, s32[32]{0:T(128)} %llen_ref.3, s32[32,31]{1,0:T(8,128)} %labels_ref.1, ...), custom_call_target="tpu_custom_call" | custom-call | tf_op jit(solution)/shard_map/lattice/pallas_call | solution.py:373
  60.8 59.9 %combine.1 = (bf16[8,4,8,512]{3,2,1,0:T(8,128)(2,1)}, bf16[8,128,640]{2,1,0:T(8,128)(2,1)}, f32[2,512,640]{2,1,0:T(8,128)}, f32[4,640,256]{2,1,0:T(8,128)}, f32[8,8,128]{2,1,0:T(8,128)}) custom-call(bf16[8,4,8,512]{3,2,1,0:T(8,128)(2,1)} %get-tuple-element.23.frames_ref, bf16[4,32,512]{2,1,0:T(8,128)(2,1)} %get-tuple-element.24.pred_ref, ...), custom_call_target="tpu_custom_call" | custom-call | tf_op jit(solution)/shard_map/combine/pallas_call | solution.py:654
  120.7 7.0 %outputs.1 = (f32[32]{0:T(128)}, bf16[32,8,512]{2,1,0:T(8,128)(2,1)}, f32[32,32,512]{2,1,0:T(8,128)}, f32[512,640]{1,0:T(8,128)}, f32[512,640]{1,0:T(8,128)}, /*index=5*/f32[640,1024]{1,0:T(8,128)}) custom-call(s32[32]{0:T(128)} %get-tuple-element.22.place_ref, f32[8,8,128]{2,1,0:T(8,128)} %get-tuple-element.33.losses_ref, ...), custom_call_target="tpu_custom_call" | custom-call | tf_op jit(solution)/shard_map/outputs/pallas_call | solution.py:722

commit v4 on v3

--- a/solution.py
+++ b/solution.py
@@ -30,8 +30,8 @@
 
 
 def exchange_kernel(n_seq, flen_ref, llen_ref, enc_ref, pred_ref, w_enc_ref, w_pred_ref, w_out_ref,
-                    order_ref, place_ref, frames_ref, own_pred_ref, a_ref, c_ref, w_out_t_ref,
-                    key_ref, sorted_ref, send_sem, recv_sem):
+                    order_ref, place_ref, frames_ref, a_ref, c_ref, w_out_t_ref,
+                    key_ref, sorted_ref, own_pred_ref, send_sem, recv_sem):
     seq = lax.axis_index("seq")
     n_utt = enc_ref.shape[0]
     n_own = n_utt // n_seq
@@ -103,16 +103,16 @@
             jax.ShapeDtypeStruct((n_utt,), jnp.int32),
             jax.ShapeDtypeStruct((n_utt,), jnp.int32),
             jax.ShapeDtypeStruct((n_seq, n_own, t_loc, width), BF16),
-            jax.ShapeDtypeStruct((n_own, n_upos, width), BF16),
             jax.ShapeDtypeStruct((n_seq * n_own * t_loc, joint), F32),
             jax.ShapeDtypeStruct((n_own * n_upos, joint), F32),
             jax.ShapeDtypeStruct((vocab, joint), BF16),
         ),
         in_specs=[sspec()] * 2 + [vspec()] * 5,
-        out_specs=(sspec(),) * 2 + (vspec(),) * 5,
+        out_specs=(sspec(),) * 2 + (vspec(),) * 4,
         scratch_shapes=[
             pltpu.SMEM((n_utt,), jnp.int32),
             VMEM(enc_loc.shape, BF16),
+            VMEM((n_own, n_upos, width), BF16),
             pltpu.SemaphoreType.DMA((n_seq - 1,)),
             pltpu.SemaphoreType.DMA((n_seq - 1,)),
         ],
@@ -331,9 +331,10 @@
         dz = dz_ref[...]
         dh_ref[:, :joint] = jnp.dot(dz, wt_ref[...], preferred_element_type=F32)
         h = h_ref[tile_rows(i), :]
-        for y in range(gw_ref.shape[0]):
-            part = dz[:, y * gw_ref.shape[2]:(y + 1) * gw_ref.shape[2]]
-            gw_ref[y] += lax.dot_general(h, part, (((0,), (0,)), ((), ())), preferred_element_type=F32)
+        for v in range(0, n_vt, 2):
+            part = lax.dot_general(h, dz[:, v * LANES:(v + 2) * LANES], (((0,), (0,)), ((), ())), preferred_element_type=F32)
+            gw_ref[v] += part[:, :LANES]
+            gw_ref[v + 1] += part[:, LANES:]
 
     def make_sums(i, dh_ref):
         first_row = jnp.clip(i, 0, n_tiles - 1) * rows_t
@@ -363,7 +364,7 @@
     dc_ref[...] = dpred_ref[...].astype(BF16)
 
 
-def lattice(n_seq, n_data, seq_idx, order, frame_len, label_len, labels, act, pred, w_out, w_out_t, n_upos, t_loc):
+def lattice(n_seq, seq_idx, order, frame_len, label_len, labels, act, pred, w_out, w_out_t, n_upos, t_loc):
     n_own = frame_len.shape[0] // n_seq
     n_frames = n_seq * t_loc
     joint, vocab = w_out.shape
@@ -375,7 +376,7 @@
         out_shape=(
             jax.ShapeDtypeStruct(act.shape, BF16),
             jax.ShapeDtypeStruct(pred.shape, BF16),
-            jax.ShapeDtypeStruct((n_data, joint, vocab // n_data), F32),
+            jax.ShapeDtypeStruct((vocab // LANES, joint, LANES), F32),
             jax.ShapeDtypeStruct((SUB, LANES), F32),
         ),
         in_specs=[sspec()] * 4 + [vspec()] * 5,
@@ -417,59 +418,62 @@
             copy.wait_send()
 
 
+class Ring:
+    def __init__(self, me, right, left):
+        self.me, self.right, self.left = me, right, left
+        self.nxt, self.prv, self.opp = lax.rem(me + 1, RING), lax.rem(me + RING - 1, RING), lax.rem(me + 2, RING)
+
+
 class Reduce:
-    def __init__(self, copies, axis, me, acc, pair, left, right):
-        self.copies, self.acc, self.pair, self.left, self.right = copies, acc, pair, left, right
-        self.me, self.nxt, self.prv, self.opp = me, lax.rem(me + 1, RING), lax.rem(me + RING - 1, RING), lax.rem(me + 2, RING)
-        self.to_right = {axis: self.nxt}
-        self.to_left = {axis: self.prv}
-
-    def begin(self, right_dev, left_dev):
-        c, acc = self.copies, self.acc
-        self.devs = (right_dev, left_dev)
-        self.a1 = c.start(acc(self.opp, 0), self.pair(0), right_dev)
-        self.b1 = c.start(acc(self.opp, 1), self.pair(1), left_dev)
-        self.b2 = c.start(acc(self.nxt, 1), self.left(1), right_dev)
-        self.a2 = c.start(acc(self.prv, 0), self.right(0), left_dev)
+    def __init__(self, copies, ring, acc, bufs):
+        self.copies, self.ring, self.acc = copies, ring, acc
+        self.pair, self.from_left, self.from_right = bufs
+
+    def begin(self):
+        c, r, acc = self.copies, self.ring, self.acc
+        self.a1 = c.start(acc(r.opp, 0), self.pair.at[0], r.right)
+        self.b1 = c.start(acc(r.opp, 1), self.pair.at[1], r.left)
+        self.b2 = c.start(acc(r.nxt, 1), self.from_left.at[1], r.right)
+        self.a2 = c.start(acc(r.prv, 0), self.from_right.at[0], r.left)
 
     def middle(self):
-        c, acc = self.copies, self.acc
+        c, r, acc = self.copies, self.ring, self.acc
         self.a1.wait_recv()
-        add = acc(self.nxt, 0)
-        add[...] = add[...] + self.pair(0)[...]
-        self.a3 = c.start(add, self.left(0), self.devs[0])
+        add = acc(r.nxt, 0)
+        add[...] = add[...] + self.pair[0]
+        self.a3 = c.start(add, self.from_left.at[0], r.right)
         self.b1.wait_recv()
-        add = acc(self.prv, 1)
-        add[...] = add[...] + self.pair(1)[...]
-        self.b3 = c.start(add, self.right(1), self.devs[1])
-
-    def end(self, store):
-        self.b2.wait_recv()
-        self.a3.wait_recv()
-        self.a2.wait_recv()
-        self.b3.wait_recv()
+        add = acc(r.prv, 1)
+        add[...] = add[...] + self.pair[1]
+        self.b3 = c.start(add, self.from_right.at[1], r.left)
+
+    def end(self, target):
+        for copy in (self.b2, self.a3, self.a2, self.b3):
+            copy.wait_recv()
         for half in range(2):
-            store(half, self.acc(self.me, half)[...] + self.left(half)[...] + self.right(half)[...])
+            target(half)[...] = self.acc(self.ring.me, half)[...] + self.from_left[half] + self.from_right[half]
 
 
 class Gather:
-    def __init__(self, copies, me, out, right_dev, left_dev):
-        self.copies, self.out, self.devs = copies, out, (right_dev, left_dev)
-        self.me, self.nxt, self.prv, self.opp = me, lax.rem(me + 1, RING), lax.rem(me + RING - 1, RING), lax.rem(me + 2, RING)
+    def __init__(self, copies, ring, out):
+        self.copies, self.ring, self.out = copies, ring, out
+
+    def send(self, k, half, device):
+        return self.copies.start(self.out(k, half), self.out(k, half), device)
 
     def begin(self):
-        c, out, (right_dev, left_dev) = self.copies, self.out, self.devs
-        self.ra = c.start(out(self.me, 0), out(self.me, 0), right_dev)
-        self.lb = c.start(out(self.me, 1), out(self.me, 1), left_dev)
-        self.rb = c.start(out(self.me, 1), out(self.me, 1), right_dev)
-        self.la = c.start(out(self.me, 0), out(self.me, 0), left_dev)
+        r = self.ring
+        self.ra = self.send(r.me, 0, r.right)
+        self.lb = self.send(r.me, 1, r.left)
+        self.rb = self.send(r.me, 1, r.right)
+        self.la = self.send(r.me, 0, r.left)
 
     def relay(self):
-        c, out, (right_dev, left_dev) = self.copies, self.out, self.devs
+        r = self.ring
         self.ra.wait_recv()
-        self.ra2 = c.start(out(self.prv, 0), out(self.prv, 0), right_dev)
+        self.ra2 = self.send(r.prv, 0, r.right)
         self.lb.wait_recv()
-        self.lb2 = c.start(out(self.nxt, 1), out(self.nxt, 1), left_dev)
+        self.lb2 = self.send(r.nxt, 1, r.left)
         self.rb.wait_recv()
         self.la.wait_recv()
 
@@ -478,218 +482,244 @@
         self.lb2.wait_recv()
 
 
-def combine_kernel(n_seq, n_data, frames_ref, pred_ref, w_enc_ref, da_ref, dc_ref, gw_ref, loss_ref,
-                   ge_out, dc_out, gj_out, gw_out, loss_out,
-                   gj_acc, gw_acc, gj_pair, gw_pair, gj_py, gj_ly, gj_ry, gj_px, gj_lx, gj_rx, gw_px, gw_lx, gw_rx, gw_py, gw_ly, gw_ry, gj_mid, gw_mid, ge_ref,
-                   send_sem, recv_sem):
+def rows_of(start, size):
+    return pl.ds(pl.multiple_of(start, SUB), size)
+
+
+def combine_kernel(n_seq, order_ref, frames_ref, pred_ref, w_enc_ref, da_ref, dc_ref, gw_ref, loss_ref,
+                   ge_out, dc_out, gwe_out, gwp_out, gwo_out, loss_out, *scratch):
+    (enc_acc, enc_pair, enc_mid, enc_y, enc_x, outs_acc, outs_pair, outs_mid, outs_1, outs_2, pred_acc, pred_y, rows_ref, ge_ref, send_sem, recv_sem) = unflatten(scratch)
     seq = lax.axis_index("seq")
     y = lax.axis_index("data")
     x = lax.div(seq, CORES)
     core = lax.rem(seq, CORES)
-    x_right = {"seq": lax.rem(x + 1, RING) * CORES + core}
-    x_left = {"seq": lax.rem(x + RING - 1, RING) * CORES + core}
-    y_right = {"data": lax.rem(y + 1, RING)}
-    y_left = {"data": lax.rem(y + RING - 1, RING)}
     mate = {"seq": x * CORES + 1 - core}
+    ring_x = Ring(x, {"seq": lax.rem(x + 1, RING) * CORES + core}, {"seq": lax.rem(x + RING - 1, RING) * CORES + core})
+    ring_y = Ring(y, {"data": lax.rem(y + 1, RING)}, {"data": lax.rem(y + RING - 1, RING)})
     barrier = pltpu.get_barrier_semaphore()
     for hop in range(1, n_seq):
         pl.semaphore_signal(barrier, inc=1, device_id={"seq": lax.rem(seq + hop, n_seq)}, device_id_type=MESH)
-    for dev in (y_right, y_left):
+    for dev in (ring_y.right, ring_y.left):
         pl.semaphore_signal(barrier, inc=1, device_id=dev, device_id_type=MESH)
 
+    n_blk = gw_ref.shape[0] // 2
+    n_utt = n_seq * frames_ref.shape[1]
+    n_upos = pred_ref.shape[1]
+    enc_half = enc_acc.shape[0] // CORES
+    out_half = gw_ref.shape[1] // CORES
+    enc_q, out_q = enc_half // RING, out_half // RING
+    enc_s = enc_q // RING
+    enc_row, out_row = core * enc_half, core * out_half
+    contract_rows = (((0,), (0,)), ((), ()))
+
     frames = frames_ref[...]
-    contract_rows = (((0,), (0,)), ((), ()))
-    gj_acc[0] = lax.dot_general(frames.reshape(-1, frames.shape[-1]), da_ref[...], contract_rows, preferred_element_type=F32)
-    own_pred = pred_ref[...]
-    gj_acc[1] = lax.dot_general(own_pred.reshape(-1, own_pred.shape[-1]), dc_ref[...], contract_rows, preferred_element_type=F32)
+    enc_acc[...] = lax.dot_general(frames.reshape(-1, frames.shape[-1]), da_ref[...], contract_rows, preferred_element_type=F32)
+    dc_out[pl.ds(seq, 1)] = dc_ref[...][None]
+    loss_out[pl.ds(seq, 1)] = loss_ref[...][None]
+    pl.semaphore_wait(barrier, n_seq - 1 + 2)
+
+    copies = Copies(send_sem, recv_sem)
+
+    def swap_out(part):
+        blocks = pl.ds(part * n_blk, n_blk)
+        return copies.start(gw_ref.at[blocks, rows_of((1 - core) * out_half, out_half), :], outs_pair[part], mate)
+
+    dc_half = dc_out.shape[1] // 2
+    dc_gather = Gather(copies, ring_x, lambda k, half: dc_out.at[k * CORES + core, pl.ds(half * dc_half, dc_half), :])
+    swap_1 = swap_out(1)
+    swap_enc = copies.start(enc_acc.at[rows_of((1 - core) * enc_half, enc_half), :], enc_pair, mate)
+    dc_gather.begin()
+    dc_mate = [copies.start(dc_out.at[seq], dc_out.at[seq], mate)]
+    swap_0 = swap_out(0)
+
+    def dc_pass(k):
+        dc_mate.append(copies.start(dc_out.at[k * CORES + core], dc_out.at[k * CORES + core], mate))
+
     ge = lax.dot_general(da_ref[...], w_enc_ref[...], (((1,), (1,)), ((), ())), preferred_element_type=F32)
     ge_ref[...] = ge.astype(BF16).reshape(ge_ref.shape)
     ge_out[pl.ds(seq, 1)] = ge_ref[pl.ds(seq, 1)]
-    dc_out[pl.ds(seq, 1)] = dc_ref[...][None]
-    loss_out[pl.ds(seq, 1)] = loss_ref[...][None]
-    pl.semaphore_wait(barrier, n_seq - 1 + 2)
-
-    copies = Copies(send_sem, recv_sem)
-    gj_half = gj_acc.shape[1] // CORES
-    gw_half = gw_ref.shape[1] // CORES
-    gj_y, gw_x = gj_half // RING, gw_half // RING
-    gj_x = gj_y // RING
-
-    mate_gj = copies.start(gj_acc.at[:, pl.ds((1 - core) * gj_half, gj_half), :], gj_pair, mate)
-    mate_gw = copies.start(gw_ref.at[:, pl.ds((1 - core) * gw_half, gw_half), :], gw_pair, mate)
-
-    dc_half = dc_out.shape[1] // 2
-
-    def dc_at(k, half):
-        return dc_out.at[k * CORES + core, pl.ds(half * dc_half, dc_half), :]
-
-    dc_gather = Gather(copies, x, dc_at, x_right, x_left)
-    dc_gather.begin()
-    dc_mate = [copies.start(dc_out.at[seq], dc_out.at[seq], mate)]
+
+    def add_out(part):
+        outs_acc[part][...] = gw_ref[pl.ds(part * n_blk, n_blk), rows_of(out_row, out_half), :] + outs_pair[part][...]
+
+    def out_first(part):
+        return lambda k, half: outs_acc[part].at[:, rows_of(k * out_q + half * (out_q // 2), out_q // 2), :]
+
+    def out_second(part):
+        return lambda k, half: outs_mid[part].at[k, pl.ds(half * (out_q // 2), out_q // 2), :]
+
+    rings = ((ring_x, ring_y), (ring_y, ring_x))
+    first = [Reduce(copies, rings[part][0], out_first(part), outs_1[part]) for part in range(2)]
+    second = [Reduce(copies, rings[part][1], out_second(part), outs_2[part]) for part in range(2)]
+    enc_first = Reduce(copies, ring_y, lambda k, half: enc_acc.at[rows_of(enc_row + k * enc_q + half * (enc_q // 2), enc_q // 2), :], enc_y)
+    enc_second = Reduce(copies, ring_x, lambda k, half: enc_mid.at[rows_of(k * enc_s + half * (enc_s // 2), enc_s // 2), :], enc_x)
+    pred_first = Reduce(copies, ring_y, lambda k, half: pred_acc.at[rows_of(k * enc_s + half * (enc_s // 2), enc_s // 2), :], pred_y)
+
+    swap_1.wait_recv()
+    add_out(1)
+    first[1].begin()
+    swap_enc.wait_recv()
+    enc_acc[rows_of(enc_row, enc_half), :] = enc_acc[rows_of(enc_row, enc_half), :] + enc_pair[...]
+    enc_first.begin()
+    swap_0.wait_recv()
+    add_out(0)
+    first[0].begin()
+    dc_gather.relay()
+    dc_pass(ring_x.prv)
+    dc_pass(ring_x.nxt)
+    first[1].middle()
+    enc_first.middle()
     small = []
     for hop in range(1, n_seq):
         peer = lax.rem(seq + hop, n_seq)
+        small.append(copies.start(loss_ref, loss_out.at[seq], {"seq": peer}))
+    for hop in range(1, n_seq):
+        peer = lax.rem(seq + hop, n_seq)
         small.append(copies.start(ge_ref.at[peer], ge_out.at[seq], {"seq": peer}))
-        small.append(copies.start(loss_ref, loss_out.at[seq], {"seq": peer}))
-
-    gj_row = pl.multiple_of(core * gj_half, gj_half)
-    gw_row = pl.multiple_of(core * gw_half, gw_half)
-
-    def gj_shard_y(k, half):
-        return gj_acc.at[:, pl.ds(pl.multiple_of(gj_row + k * gj_y + half * (gj_y // 2), SUB), gj_y // 2), :]
-
-    def gw_shard_x(k, half):
-        return gw_acc.at[:, pl.ds(pl.multiple_of(k * gw_x + half * (gw_x // 2), SUB), gw_x // 2), :]
-
-    def halves(ref):
-        return lambda half: ref.at[half]
-
-    mate_gj.wait_recv()
-    gj_acc[:, pl.ds(gj_row, gj_half), :] = gj_acc[:, pl.ds(gj_row, gj_half), :] + gj_pair[...]
-    gj_r1 = Reduce(copies, "data", y, gj_shard_y, halves(gj_py), halves(gj_ly), halves(gj_ry))
-    gj_r1.begin(y_right, y_left)
-    mate_gw.wait_recv()
-    gw_acc[...] = gw_ref[:, pl.ds(gw_row, gw_half), :] + gw_pair[...]
-    gw_r1 = Reduce(copies, "seq", x, gw_shard_x, halves(gw_px), halves(gw_lx), halves(gw_rx))
-    gw_r1.begin(x_right, x_left)
-
-    dc_gather.relay()
-    dc_mate.append(copies.start(dc_out.at[dc_gather.prv * CORES + core], dc_out.at[dc_gather.prv * CORES + core], mate))
-    dc_mate.append(copies.start(dc_out.at[dc_gather.nxt * CORES + core], dc_out.at[dc_gather.nxt * CORES + core], mate))
-    gj_r1.middle()
-    gw_r1.middle()
-
-    def keep_gj(half, value):
-        gj_mid[:, pl.ds(half * (gj_y // 2), gj_y // 2), :] = value
-
-    gj_r1.end(keep_gj)
-
-    def gj_shard_x(k, half):
-        return gj_mid.at[:, pl.ds(pl.multiple_of(k * gj_x + half * (gj_x // 2), SUB), gj_x // 2), :]
-
-    gj_r2 = Reduce(copies, "seq", x, gj_shard_x, halves(gj_px), halves(gj_lx), halves(gj_rx))
-    gj_r2.begin(x_right, x_left)
-
-    def keep_gw(half, value):
-        gw_mid[:, pl.ds(half * (gw_x // 2), gw_x // 2), :] = value
-
-    gw_r1.end(keep_gw)
-
-    def gw_shard_y(k, half):
-        return gw_mid.at[k, pl.ds(half * (gw_x // 2), gw_x // 2), :]
-
-    gw_r2 = Reduce(copies, "data", y, gw_shard_y, halves(gw_py), halves(gw_ly), halves(gw_ry))
-    gw_r2.begin(y_right, y_left)
-    gj_r2.middle()
-    gw_r2.middle()
-
-    def gj_out_x(k, half):
-        return gj_out.at[:, pl.ds(pl.multiple_of(gj_row + y * gj_y + k * gj_x + half * (gj_x // 2), SUB), gj_x // 2), :]
-
-    def gw_out_y(k, half):
-        return gw_out.at[k, pl.ds(pl.multiple_of(gw_row + x * gw_x + half * (gw_x // 2), SUB), gw_x // 2), :]
-
-    def put_gj(half, value):
-        gj_out_x(x, half)[...] = value
-
-    def put_gw(half, value):
-        gw_out_y(y, half)[...] = value
-
-    gj_r2.end(put_gj)
-    gj_g1 = Gather(copies, x, gj_out_x, x_right, x_left)
-    gj_g1.begin()
-    gw_r2.end(put_gw)
-    gw_g1 = Gather(copies, y, gw_out_y, y_right, y_left)
-    gw_g1.begin()
-    gj_g1.relay()
-    gw_g1.relay()
-    gj_g1.finish()
-
-    def gj_out_y(k, half):
-        return gj_out.at[:, pl.ds(pl.multiple_of(gj_row + k * gj_y + half * (gj_y // 2), SUB), gj_y // 2), :]
-
-    def gw_out_x(k, half):
-        return gw_out.at[:, pl.ds(pl.multiple_of(gw_row + k * gw_x + half * (gw_x // 2), SUB), gw_x // 2), :]
-
-    gj_g2 = Gather(copies, y, gj_out_y, y_right, y_left)
-    gj_g2.begin()
-    gw_g1.finish()
-    gw_g2 = Gather(copies, x, gw_out_x, x_right, x_left)
-    gw_g2.begin()
-
-    def gj_whole(k):
-        return gj_out.at[:, pl.ds(pl.multiple_of(gj_row + k * gj_y, SUB), gj_y), :]
-
-    def gw_whole(k):
-        return gw_out.at[:, pl.ds(pl.multiple_of(gw_row + k * gw_x, SUB), gw_x), :]
-
-    last = [copies.start(gj_whole(y), gj_whole(y), mate), copies.start(gw_whole(x), gw_whole(x), mate)]
+    first[0].middle()
     dc_gather.finish()
-    dc_mate.append(copies.start(dc_out.at[dc_gather.opp * CORES + core], dc_out.at[dc_gather.opp * CORES + core], mate))
-    gj_g2.relay()
-    for k in (gj_g2.prv, gj_g2.nxt):
-        last.append(copies.start(gj_whole(k), gj_whole(k), mate))
-    gw_g2.relay()
-    for k in (gw_g2.prv, gw_g2.nxt):
-        last.append(copies.start(gw_whole(k), gw_whole(k), mate))
-    gj_g2.finish()
-    last.append(copies.start(gj_whole(gj_g2.opp), gj_whole(gj_g2.opp), mate))
-    gw_g2.finish()
-    last.append(copies.start(gw_whole(gw_g2.opp), gw_whole(gw_g2.opp), mate))
-    for copy in small + dc_mate + last:
+    dc_pass(ring_x.opp)
+
+    def out_place(part, k1, k2, half, whole=False):
+        start, size = out_row + k1 * out_q, out_q
+        if not whole:
+            start, size = start + half * (out_q // 2), out_q // 2
+        return gwo_out.at[part * n_blk + k2 if k2 is not None else pl.ds(part * n_blk, n_blk), rows_of(start, size), :]
+
+    first[1].end(lambda half: outs_mid[1].at[:, pl.ds(half * (out_q // 2), out_q // 2), :])
+    second[1].begin()
+    enc_first.end(lambda half: enc_mid.at[pl.ds(half * (enc_q // 2), enc_q // 2), :])
+    enc_second.begin()
+
+    for copy in dc_mate:
+        copy.wait_recv()
+    for k in range(n_utt):
+        rows_ref[k * n_upos:(k + 1) * n_upos, :] = pred_ref[order_ref[k], :, pl.ds(pl.multiple_of(x * LANES, LANES), LANES)]
+    pred_part = lax.dot_general(rows_ref[...], dc_out[...].reshape(n_utt * n_upos, -1), contract_rows, preferred_element_type=F32)
+    pred_acc[...] = jnp.where(core == 0, pred_part[:enc_q], pred_part[enc_q:])
+    pred_first.begin()
+
+    first[0].end(lambda half: outs_mid[0].at[:, pl.ds(half * (out_q // 2), out_q // 2), :])
+    second[0].begin()
+    second[1].middle()
+    enc_second.middle()
+    pred_first.middle()
+    second[0].middle()
+
+    def pair_place(part):
+        ring1, ring2 = rings[part]
+        return (
+            Gather(copies, ring2, lambda k, half: out_place(part, ring1.me, k, half)),
+            Gather(copies, ring1, lambda k, half: out_place(part, k, None, half)),
+        )
+
+    gathers = [pair_place(0), pair_place(1)]
+    enc_at = lambda ky, kx, half: gwe_out.at[rows_of(enc_row + ky * enc_q + kx * enc_s + half * (enc_s // 2), enc_s // 2), :]
+    enc_g1 = Gather(copies, ring_x, lambda k, half: enc_at(y, k, half))
+    enc_g2 = Gather(copies, ring_y, lambda k, half: gwe_out.at[rows_of(enc_row + k * enc_q + half * (enc_q // 2), enc_q // 2), :])
+    pred_at = lambda ky, half: gwp_out.at[x, core, rows_of(ky * enc_s + half * (enc_s // 2), enc_s // 2), :]
+    pred_g1 = Gather(copies, ring_y, pred_at)
+    pred_g2 = Gather(copies, ring_x, lambda k, half: gwp_out.at[k, core, pl.ds(half * (enc_q // 2), enc_q // 2), :])
+
+    second[1].end(lambda half: out_place(1, y, x, half))
+    gathers[1][0].begin()
+    enc_second.end(lambda half: enc_at(y, x, half))
+    enc_g1.begin()
+    pred_first.end(lambda half: pred_at(y, half))
+    pred_g1.begin()
+    second[0].end(lambda half: out_place(0, x, y, half))
+    gathers[0][0].begin()
+    gathers[1][0].relay()
+    enc_g1.relay()
+    pred_g1.relay()
+    gathers[0][0].relay()
+
+    last = []
+
+    def pass_on(ref):
+        last.append(copies.start(ref, ref, mate))
+
+    enc_whole = lambda k: gwe_out.at[rows_of(enc_row + k * enc_q, enc_q), :]
+    pred_whole = lambda k: gwp_out.at[k, core]
+    out_whole = lambda part: lambda k: out_place(part, k, None, 0, True)
+    finals = [(gathers[1], out_whole(1)), ((enc_g1, enc_g2), enc_whole), ((pred_g1, pred_g2), pred_whole), (gathers[0], out_whole(0))]
+    for (g1, g2), whole in finals:
+        g1.finish()
+        g2.begin()
+        pass_on(whole(g2.ring.me))
+    for (g1, g2), whole in finals:
+        g2.relay()
+        pass_on(whole(g2.ring.prv))
+        pass_on(whole(g2.ring.nxt))
+    for (g1, g2), whole in finals:
+        g2.finish()
+        pass_on(whole(g2.ring.opp))
+    for copy in small + last:
         copy.wait_recv()
     copies.drain()
 
 
-N_COPIES = 6 + 2 + 4 + 14 + 4 * 6 + 4 * 6 + 8
-
-
-def combine(n_seq, n_data, frames, own_pred, w_enc, da, dc, gw, loss):
+N_COPIES = 3 + 10 + 14 + 6 * 7 + 6 * 8 + 16
+
+
+def unflatten(refs):
+    refs = list(refs)
+    take = lambda n: [refs.pop(0) for _ in range(n)]
+    enc_acc, enc_pair, enc_mid = take(3)
+    enc_y, enc_x = take(3), take(3)
+    outs = [(take(1)[0], take(1)[0], take(1)[0], take(3), take(3)) for _ in range(2)]
+    outs_acc, outs_pair, outs_mid, outs_1, outs_2 = zip(*outs)
+    pred_acc = refs.pop(0)
+    pred_y = take(3)
+    return (enc_acc, enc_pair, enc_mid, enc_y, enc_x, outs_acc, outs_pair, outs_mid, outs_1, outs_2, pred_acc, pred_y, *refs)
+
+
+def combine(n_seq, order, frames, pred_loc, w_enc, da, dc, gw, loss):
     width = frames.shape[-1]
+    n_utt, n_upos, _ = pred_loc.shape
     joint = da.shape[-1]
-    n_cols, _, col = gw.shape
-    gj_half, gw_half = width // CORES, joint // CORES
-    gj_y, gw_x = gj_half // RING, gw_half // RING
-    gj_x = gj_y // RING
+    n_blk = gw.shape[0] // 2
+    enc_half, out_half = width // CORES, joint // CORES
+    enc_q, out_q = enc_half // RING, out_half // RING
+    enc_s = enc_q // RING
+    ring = lambda *shape: [VMEM(shape, F32)] * 3
+    outs = [VMEM((n_blk, out_half, LANES), F32)] * 2 + [VMEM((n_blk, out_q, LANES), F32)] + ring(2, n_blk, out_q // 2, LANES) + ring(2, out_q // 2, LANES)
     return pl.pallas_call(
-        functools.partial(combine_kernel, n_seq, n_data),
+        functools.partial(combine_kernel, n_seq),
         out_shape=(
             jax.ShapeDtypeStruct(frames.shape, BF16),
             jax.ShapeDtypeStruct((n_seq,) + dc.shape, BF16),
-            jax.ShapeDtypeStruct((2, width, joint), F32),
+            jax.ShapeDtypeStruct((width, joint), F32),
+            jax.ShapeDtypeStruct((RING, CORES, enc_q, joint), F32),
             jax.ShapeDtypeStruct(gw.shape, F32),
             jax.ShapeDtypeStruct((n_seq,) + loss.shape, F32),
         ),
-        in_specs=[vspec()] * 7,
-        out_specs=(vspec(),) * 5,
-        scratch_shapes=[
-            VMEM((2, width, joint), F32),
-            VMEM((n_cols, gw_half, col), F32),
-            VMEM((2, gj_half, joint), F32),
-            VMEM((n_cols, gw_half, col), F32),
-        ]
-        + [VMEM((2, 2, gj_y // 2, joint), F32)] * 3
-        + [VMEM((2, 2, gj_x // 2, joint), F32)] * 3
-        + [VMEM((2, n_cols, gw_x // 2, col), F32)] * 3
-        + [VMEM((2, gw_x // 2, col), F32)] * 3
+        in_specs=[sspec()] + [vspec()] * 7,
+        out_specs=(vspec(),) * 6,
+        scratch_shapes=[VMEM((width, joint), F32), VMEM((enc_half, joint), F32), VMEM((enc_q, joint), F32)]
+        + ring(2, enc_q // 2, joint)
+        + ring(2, enc_s // 2, joint)
+        + outs
+        + outs
+        + [VMEM((enc_q, joint), F32)]
+        + ring(2, enc_s // 2, joint)
         + [
-            VMEM((2, gj_y, joint), F32),
-            VMEM((n_cols, gw_x, col), F32),
+            VMEM((n_utt * n_upos, LANES), BF16),
             VMEM(frames.shape, BF16),
             pltpu.SemaphoreType.DMA((N_COPIES,)),
             pltpu.SemaphoreType.DMA((N_COPIES,)),
         ],
         compiler_params=pltpu.CompilerParams(collective_id=1, has_side_effects=True, vmem_limit_bytes=VMEM_LIMIT),
         name="combine",
-    )(frames, own_pred, w_enc, da, dc, gw, loss)
-
-
-def output_kernel(place_ref, losses_ref, ge_ref, dc_ref, w_pred_ref, gj_ref, gw_ref,
+    )(order, frames, pred_loc, w_enc, da, dc, gw, loss)
+
+
+def output_kernel(place_ref, losses_ref, ge_ref, dc_ref, w_pred_ref, gwe_ref, gwp_ref, gw_ref,
                   loss_out, ge_out, gp_out, gwe_out, gwp_out, gwo_out, rows_ref, gp_ref, sem):
     n_utt, n_upos, width = gp_out.shape
     n_own = ge_ref.shape[1]
     n_cols, _, col = gw_ref.shape
-    copies = [pltpu.make_async_copy(gj_ref.at[0], gwe_out, sem.at[0]), pltpu.make_async_copy(gj_ref.at[1], gwp_out, sem.at[1])]
+    copies = [pltpu.make_async_copy(gwe_ref, gwe_out, sem.at[0]), pltpu.make_async_copy(gwp_ref, gwp_out, sem.at[1])]
     for k in range(n_cols):
         copies.append(pltpu.make_async_copy(gw_ref.at[k], gwo_out.at[:, pl.ds(k * col, col)], sem.at[2 + k]))
     for copy in copies:
@@ -714,7 +744,7 @@
         copy.wait()
 
 
-def outputs(place, losses, ge, dc, w_pred, gj, gw, n_upos):
+def outputs(place, losses, ge, dc, w_pred, gwe, gwp, gw, n_upos):
     n_seq, n_own, t_loc, width = ge.shape
     n_utt = n_seq * n_own
     n_cols, joint, col = gw.shape
@@ -729,7 +759,7 @@
             jax.ShapeDtypeStruct((width, joint), F32),
             jax.ShapeDtypeStruct((joint, n_cols * col), F32),
         ),
-        in_specs=[sspec()] * 2 + [vspec()] * 5,
+        in_specs=[sspec()] * 2 + [vspec()] * 6,
         out_specs=(sspec(), vspec()) + (hbm,) * 4,
         scratch_shapes=[
             VMEM((n_utt, n_upos, joint), BF16),
@@ -738,12 +768,11 @@
         ],
         compiler_params=pltpu.CompilerParams(vmem_limit_bytes=VMEM_LIMIT),
         name="outputs",
-    )(place, losses, ge, dc, w_pred, gj, gw)
+    )(place, losses, ge, dc, w_pred, gwe, gwp, gw)
 
 
 def solution(mesh):
     n_seq = mesh.shape["seq"]
-    n_data = mesh.shape["data"]
     utt_rows = P(("part", "data"))
     utt_mats = P(("part", "data"), None)
     utt_cube = P(("part", "data"), None, None)
@@ -755,10 +784,10 @@
         t_loc = enc_loc.shape[1]
         n_upos = pred_loc.shape[1]
         seq_idx = lax.axis_index("seq").astype(jnp.int32).reshape(1)
-        order, place, frames, own_pred, act, pred, w_out_t = exchange(n_seq, frame_len, label_len, enc_loc, pred_loc, w_enc, w_pred, w_out)
-        da, dc, gw, loss = lattice(n_seq, n_data, seq_idx, order, frame_len, label_len, labels, act, pred, w_out, w_out_t, n_upos, t_loc)
-        ge, dc_all, gj, gw, losses = combine(n_seq, n_data, frames, own_pred, w_enc, da, dc, gw, loss)
-        loss, grad_enc, grad_pred, gw_enc, gw_pred, gw_out = outputs(place, losses, ge, dc_all, w_pred, gj, gw, n_upos)
+        order, place, frames, act, pred, w_out_t = exchange(n_seq, frame_len, label_len, enc_loc, pred_loc, w_enc, w_pred, w_out)
+        da, dc, gw, loss = lattice(n_seq, seq_idx, order, frame_len, label_len, labels, act, pred, w_out, w_out_t, n_upos, t_loc)
+        ge, dc_all, gwe, gwp, gw, losses = combine(n_seq, order, frames, pred_loc, w_enc, da, dc, gw, loss)
+        loss, grad_enc, grad_pred, gw_enc, gw_pred, gw_out = outputs(place, losses, ge, dc_all, w_pred, gwe, gwp.reshape(gwe.shape), gw, n_upos)
         return loss, grad_enc, grad_pred, gw_enc, gw_pred, gw_out
 
     return jax.shard_map(body, mesh=mesh, in_specs=(enc_spec, utt_cube, weight_in, weight_in, weight_in, utt_mats, utt_rows, utt_rows), out_specs=(utt_rows, enc_spec, utt_cube, weight_out, weight_out, weight_out), check_vma=False)

time: 127 us -> 123 us (0.969); the launches traced: 128 us -> 120 us
  Pallas kernels: 127 us -> 120 us
    pallas_call x1, Pallas kernels: 59.9 us -> 52.6 us  [combine(): pl.pallas_call(functools.partial(combine_kernel, n_seq), out_shape=(jax.S...]
where the time goes in v4:
time: 123 us; the launch traced here: 120 us
  Pallas kernels  120 us (98%)
    pallas_call x1, Pallas kernels, combine(): pl.pallas_call(functools.partial(combine_kernel, n_seq), out_shape=(jax.S...  52.6 us
    pallas_call x1, Pallas kernels, lattice(): pl.pallas_call(functools.partial(lattice_kernel, n_own, n_frames, n_upos)...  44.6 us
    pallas_call x1, Pallas kernels, exchange(): pl.pallas_call(functools.partial(exchange_kernel, n_seq), out_shape=(jax....  15.5 us
    pallas_call x1, Pallas kernels, outputs(): pl.pallas_call(output_kernel, out_shape=(jax.ShapeDtypeStruct((n_utt,), F...  7.03 us

profile of v4, /device:TPU:97, one launch (start us, length us, event | category | flops | bytes accessed | tf_op | source)
XLA Modules:
  0.0 120.4 jit_solution(10237338314911652786)
XLA Ops:
  0.6 15.5 %exchange.1 = (s32[32]{0:T(128)}, s32[32]{0:T(128)}, bf16[8,4,8,512]{3,2,1,0:T(8,128)(2,1)}, f32[256,640]{1,0:T(8,128)}, f32[128,640]{1,0:T(8,128)}, /*index=5*/bf16[1024,640]{1,0:T(8,128)(2,1)}) custom-call(s32[32]{0:T(128)} %flen_ref.3, s32[32]{0:T(128)} %llen_ref.3, bf16[32,8,512]{2,1,0:T(8,128)(2,1)} %enc_ref.1, bf16[32,32,512]{2,1,0:T(8,128)(2,1)} %pred_ref.3, ...), custom_call_target="tpu_custom_call" | custom-call | tf_op jit(solution)/shard_map/exchange/pallas_call | solution.py:100
  16.1 44.6 %lattice.1 = (bf16[256,640]{1,0:T(8,128)(2,1)}, bf16[128,640]{1,0:T(8,128)(2,1)}, f32[8,640,128]{2,1,0:T(8,128)}, f32[8,128]{1,0:T(8,128)}) custom-call(s32[1]{0:T(128)} %bitcast.seq_ref, s32[32]{0:T(128)} %get-tuple-element.23.order_ref, s32[32]{0:T(128)} %flen_ref.3, s32[32]{0:T(128)} %llen_ref.3, s32[32,31]{1,0:T(8,128)} %labels_ref.1, ...), custom_call_target="tpu_custom_call" | custom-call | tf_op jit(solution)/shard_map/lattice/pallas_call | solution.py:374
  60.7 52.6 %combine.1 = (bf16[8,4,8,512]{3,2,1,0:T(8,128)(2,1)}, bf16[8,128,640]{2,1,0:T(8,128)(2,1)}, f32[512,640]{1,0:T(8,128)}, f32[4,2,64,640]{3,2,1,0:T(8,128)}, f32[8,640,128]{2,1,0:T(8,128)}, /*index=5*/f32[8,8,128]{2,1,0:T(8,128)}) custom-call(s32[32]{0:T(128)} %get-tuple-element.23.order_ref, bf16[8,4,8,512]{3,2,1,0:T(8,128)(2,1)} %get-tuple-element.24.frames_ref, ...), custom_call_target="tpu_custom_call" | custom-call | tf_op jit(solution)/shard_map/combine/pallas_call | solution.py:687
  113.3 7.0 %outputs.1 = (f32[32]{0:T(128)}, bf16[32,8,512]{2,1,0:T(8,128)(2,1)}, f32[32,32,512]{2,1,0:T(8,128)}, f32[512,640]{1,0:T(8,128)}, f32[512,640]{1,0:T(8,128)}, /*index=5*/f32[640,1024]{1,0:T(8,128)}) custom-call(s32[32]{0:T(128)} %get-tuple-element.22.place_ref, f32[8,8,128]{2,1,0:T(8,128)} %get-tuple-element.32.losses_ref, ...), custom_call_target="tpu_custom_call" | custom-call | tf_op jit(solution)/shard_map/outputs/pallas_call | solution.py:752
